TPU v7x, 32 devices: a whole 2x2x4 slice. The times are simulated.
32 devices in a mesh: tp: 4 (over z), dp: 8 (over y, x, core).
Axes of the slice: x: 2, y: 2, z: 4, core: 2. Of those that a mesh axis runs over, the one named last changes fastest.
Arguments:
- feats: bfloat16 [4096, 49, 768], P('dp')
- ln_gamma: float32 [768], replicated
- ln_beta: float32 [768], replicated
- w_head: bfloat16 [768, 22528], P(None, 'tp')
- b_head: float32 [22528], P('tp')
- labels: int32 [4096], P('dp')
Outputs:
- output 1: float32 [], replicated
- output 2: bfloat16 [4096, 49, 768], P('dp')
- output 3: float32 [768, 22528], P(None, 'tp')
- output 4: float32 [22528], P('tp')
- output 5: float32 [768], replicated
- output 6: float32 [768], replicated
All inputs are finite; a program needn't handle non-finite values.
Results may differ from a plain program's by a relative error of at most 0.001.
Values sent between devices are 32-bit elements.
A program may use at most 1 GiB of HBM per device.

v0:
```python
import jax
import jax.numpy as jnp
from jax import lax
from jax.sharding import PartitionSpec as P

VALID_CLASSES = 21841
LN_EPS = 1e-5
SMOOTH = 0.1


def norm_pool(feats, ln_gamma, ln_beta):
    x_val = feats.astype(jnp.float32)
    mean_x = jnp.mean(x_val, axis=-1, keepdims=True)
    centered = x_val - mean_x
    var_x = jnp.mean(centered * centered, axis=-1, keepdims=True)
    inv_std = lax.rsqrt(var_x + LN_EPS)
    x_hat = centered * inv_std
    x_hat_mean = jnp.mean(x_hat, axis=1)
    pooled16 = (x_hat_mean * ln_gamma + ln_beta).astype(jnp.bfloat16)
    return x_hat, inv_std, x_hat_mean, pooled16


def norm_backward(grad_pool, x_hat, inv_std, x_hat_mean, ln_gamma):
    token_count = x_hat.shape[1]
    grad_gamma = jnp.sum(grad_pool * x_hat_mean, axis=0)
    grad_beta = jnp.sum(grad_pool, axis=0)
    upstream = grad_pool * ln_gamma / token_count
    up_mean = jnp.mean(upstream, axis=-1)
    proj_term = jnp.mean(x_hat * upstream[:, None, :], axis=-1, keepdims=True)
    grad_x = inv_std * (upstream[:, None, :] - up_mean[:, None, None] - x_hat * proj_term)
    return grad_x.astype(jnp.bfloat16), grad_gamma, grad_beta


def solution(mesh):
    data_size = mesh.shape["dp"]

    def local_head(feats, ln_gamma, ln_beta, w_head, b_head, labels):
        shard_cols = w_head.shape[1]
        global_rows = feats.shape[0] * data_size
        x_hat, inv_std, x_hat_mean, pooled16 = norm_pool(feats, ln_gamma, ln_beta)
        col_ids = lax.axis_index("tp") * shard_cols + jnp.arange(shard_cols)
        valid_mask = col_ids < VALID_CLASSES
        logits = jnp.dot(pooled16, w_head, preferred_element_type=jnp.float32) + b_head
        logits = jnp.where(valid_mask, logits, -1e30)
        row_max = lax.pmax(jnp.max(logits, axis=-1), "tp")
        shifted = jnp.exp(logits - row_max[:, None])
        onehot = col_ids == labels[:, None]
        row_stats = jnp.stack([jnp.sum(shifted, axis=-1), jnp.sum(jnp.where(onehot, logits, 0.0), axis=-1), jnp.sum(jnp.where(valid_mask, logits, 0.0), axis=-1)])
        row_stats = lax.psum(row_stats, "tp")
        log_norm = row_max + jnp.log(row_stats[0])
        loss_rows = log_norm - (1.0 - SMOOTH) * row_stats[1] - (SMOOTH / VALID_CLASSES) * row_stats[2]
        soft_probs = shifted / row_stats[0][:, None]
        dlogit = (soft_probs - (1.0 - SMOOTH) * onehot - (SMOOTH / VALID_CLASSES) * valid_mask) / global_rows
        dlogit16 = dlogit.astype(jnp.bfloat16)
        grad_w = lax.psum(lax.dot_general(pooled16, dlogit16, (((0,), (0,)), ((), ())), preferred_element_type=jnp.float32), "dp")
        grad_b = lax.psum(jnp.sum(dlogit, axis=0), "dp")
        grad_pool = lax.dot_general(dlogit16, w_head, (((1,), (1,)), ((), ())), preferred_element_type=jnp.float32)
        grad_pool = lax.psum(grad_pool, "tp")
        grad_feats, grad_gamma, grad_beta = norm_backward(grad_pool, x_hat, inv_std, x_hat_mean, ln_gamma)
        loss_sum, grad_gamma, grad_beta = lax.psum((jnp.sum(loss_rows), grad_gamma, grad_beta), "dp")
        return loss_sum / global_rows, grad_feats, grad_w, grad_b, grad_gamma, grad_beta

    return jax.shard_map(local_head, mesh=mesh, in_specs=(P("dp", None, None), P(), P(), P(None, "tp"), P("tp"), P("dp")), out_specs=(P(), P("dp", None, None), P(None, "tp"), P("tp"), P(), P()), check_vma=False)
```

profile of v0, /device:TPU:0, one launch (start us, length us, event | category | flops | bytes accessed | tf_op | source)
XLA Modules:
  0.0 425.4 jit_solution(5836579341429526393)
XLA Ops:
  7.2 0.0 all-reduce.4.cloned.1.call-start
  7.3 0.7 broadcast_multiply_fusion.2
  8.0 12.6 %convert_reduce_fusion = f32[512,49]{0,1:T(8,128)S(1)} fusion(bf16[512,49,768]{2,0,1:T(8,128)(2,1)} %param.6), kind=kLoop, calls=%fused_computation.1 | loop fusion | flops 38510080 | bytes 38635520 | tf_op jit(solution)/shard_map/reduce_sum | solution.py:13
  20.6 16.7 %fusion.9 = f32[512,49]{0,1:T(8,128)S(1)} fusion(bf16[512,49,768]{2,0,1:T(8,128)(2,1)} %param.6, f32[512,49]{0,1:T(8,128)S(1)} %broadcast_multiply_fusion.1), kind=kLoop, calls=%fused_computation.11 | loop fusion | flops 77045248 | bytes 38735872 | tf_op jit(solution)/shard_map/reduce_sum | solution.py:15
  37.3 0.0 copy-start.1
  37.3 0.0 copy-start.4
  37.4 14.8 %fusion.4 = f32[512,768]{1,0:T(8,128)S(1)} fusion(bf16[512,49,768]{2,0,1:T(8,128)(2,1)} %param.6, f32[512,49]{0,1:T(8,128)S(1)} %add_rsqrt_fusion, f32[512,49]{0,1:T(8,128)S(1)} %broadcast_multiply_fusion.1), kind=kLoop, calls=%fused_computation.6 | loop fusion | flops 76677120 | bytes 40308736 | tf_op jit(solution)/shard_map/reduce_sum | solution.py:18
  52.1 0.0 copy-done.1
  52.2 0.0 copy-done.4
  52.2 0.0 copy-start.3
  52.2 11.1 %fusion.24 = (f32[512]{0:T(512)S(1)}, f32[512,5632]{1,0:T(8,128)}) fusion(f32[5632]{0:T(1024)S(1)} %copy-done.4, bf16[768,5632]{1,0:T(8,128)(2,1)} %param.9, f32[512,768]{1,0:T(8,128)S(1)} %fusion.4, f32[768]{0:T(1024)S(1)} %copy-done.1, f32[768]{0:T(1024)S(1)} %broadcast_multiply_fusion.2, pred[5632]{0:T(1024)(128)(4,1)S(1)} %broadcast_compare_fusion), kind=kOutput, calls=%fused_computation.46 | convolution fusion | flops 4439014912 | bytes 21794304 | tf_op jit(solution)/shard_map/dot_general | solution.py:43
  63.2 13.5 %pmax.7 = f32[512]{0:T(512)S(1)} all-reduce(f32[512]{0:T(512)S(1)} %get-tuple-element.24), channel_id=1, replica_groups=mesh['tp'=4,'dp'=8] {'tp'}, use_global_device_ids=true, to_apply=%region_4.5 | all-reduce | flops 512 | bytes 4096 | tf_op jit(solution)/shard_map/pmax | solution.py:45
  76.7 0.0 copy-done.3
  76.7 7.2 %fusion.14 = (f32[512]{0:T(512)S(1)}, f32[512]{0:T(512)S(1)}, f32[512]{0:T(512)S(1)}) fusion(f32[512,5632]{1,0:T(8,128)} %get-tuple-element.25, f32[512]{0:T(512)S(1)} %pmax.7, pred[5632]{0:T(1024)(128)(4,1)S(1)} %broadcast_compare_fusion, s32[512]{0:T(512)S(1)} %copy-done.3, s32[5632]{0:T(1024)S(1)} %iota_add_fusion), kind=kLoop, calls=%fused_computation.21 | loop fusion | flops 20183552 | bytes 11572736 | tf_op jit(solution)/shard_map/reduce_sum | solution.py:48
  83.9 8.5 %psum.49 = f32[3,512]{1,0:T(4,128)S(1)} all-reduce(f32[3,512]{1,0:T(4,128)S(1)} %pad_maximum_fusion), channel_id=1, replica_groups=mesh['tp'=4,'dp'=8] {'tp'}, use_global_device_ids=true, to_apply=%region_8.9 | all-reduce | flops 1536 | bytes 12288 | tf_op jit(solution)/shard_map/psum | solution.py:49
  92.4 7.6 %fusion.21 = (f32[5632]{0:T(1024)S(1)}, bf16[512,5632]{1,0:T(8,128)(2,1)S(1)}) fusion(f32[5632]{0:T(1024)S(1)} %broadcast_select_fusion, s32[512]{0:T(512)S(1)} %copy-done.3, s32[5632]{0:T(1024)S(1)} %iota_add_fusion, f32[512]{0:T(512)S(1)} %bitcast.10, f32[512,5632]{1,0:T(8,128)} %get-tuple-element.25, f32[512]{0:T(512)S(1)} %pmax.7), kind=kLoop, calls=%fused_computation.44 | loop fusion | flops 25946624 | bytes 17375232 | tf_op jit(solution)/shard_map/reduce_sum | solution.py:56
  100.0 0.0 copy-start
  100.0 2.5 copy-done
  102.6 8.3 %fusion.17 = f32[512,768]{1,0:T(8,128)} fusion(bf16[768,5632]{1,0:T(8,128)(2,1)} %param.9, bf16[512,5632]{1,0:T(8,128)(2,1)S(1)} %get-tuple-element.18), kind=kOutput, calls=%fused_computation.24 | convolution fusion | flops 4429185024 | bytes 15990784 | tf_op jit(solution)/shard_map/dot_general | solution.py:57
  110.8 0.0 all-reduce.4.cloned.1.call-update
  110.8 0.0 all-reduce.6.cloned.1.call-start
  110.9 11.4 %fusion.15 = f32[768,5632]{1,0:T(8,128)} fusion(bf16[512,5632]{1,0:T(8,128)(2,1)} %copy-done, f32[512,768]{1,0:T(8,128)S(1)} %fusion.4, f32[768]{0:T(1024)S(1)} %copy-done.1, f32[768]{0:T(1024)S(1)} %broadcast_multiply_fusion.2), kind=kOutput, calls=%fused_computation.22 | convolution fusion | flops 4430364672 | bytes 24647680 | tf_op jit(solution)/shard_map/dot_general | solution.py:55
  122.3 0.0 copy-start.2
  122.3 0.0 all-reduce.6.cloned.1.call-update
  122.4 0.6 subtract_reduce_fusion
  123.0 56.5 %all-reduce.4.cloned.1.call-done = f32[512,768]{1,0:T(8,128)} async-done(((f32[512,768]{1,0:T(8,128)}), f32[512,768]{1,0:T(8,128)}) %all-reduce.4.cloned.1.call-update) | async-done | bytes 1572880 | tf_op jit(solution)/shard_map/psum | solution.py:58
  179.5 0.0 copy-done.2
  179.5 1.9 fusion.20
  181.3 25.7 %all-reduce = (f32[]{:T(128)}, f32[5632]{0:T(1024)}, f32[768]{0:T(1024)}, f32[768]{0:T(1024)}) all-reduce(f32[]{:T(128)} %subtract_reduce_fusion, f32[5632]{0:T(1024)S(1)} %get-tuple-element.17, f32[768]{0:T(1024)S(1)} %get-tuple-element.19, f32[768]{0:T(1024)S(1)} %get-tuple-element.20), channel_id=1, replica_groups=mesh['tp'=4,'dp'=8] {'dp'}, use_global_device_ids=true, to_apply=%region_10.11 | all-reduce | flops 7169 | bytes 57352 | tf_op jit(solution)/shard_map/psum | solution.py:60
  207.7 20.5 %fusion.5 = f32[512,49]{0,1:T(8,128)S(1)} fusion(bf16[512,49,768]{2,0,1:T(8,128)(2,1)} %param.6, f32[512,768]{1,0:T(8,128)S(1)} %get-tuple-element.16, f32[512,49]{0,1:T(8,128)S(1)} %add_rsqrt_fusion, f32[512,49]{0,1:T(8,128)S(1)} %broadcast_multiply_fusion.1), kind=kLoop, calls=%fused_computation.7 | loop fusion | flops 96312832 | bytes 40409088 | tf_op jit(solution)/shard_map/reduce_sum | solution.py:29
  228.3 0.2 broadcast_subtract_fusion
  228.5 26.2 %fusion.8 = bf16[512,49,768]{2,0,1:T(8,128)(2,1)} fusion(bf16[512,49,768]{2,0,1:T(8,128)(2,1)} %param.6, f32[512,49]{0,1:T(8,128)S(1)} %broadcast_multiply_fusion, f32[512,768]{1,0:T(8,128)S(1)} %broadcast_subtract_fusion, f32[512,49]{0,1:T(8,128)S(1)} %add_rsqrt_fusion, f32[512,49]{0,1:T(8,128)S(1)} %broadcast_multiply_fusion.1), kind=kLoop, calls=%fused_computation.10 | loop fusion | flops 134873088 | bytes 78944256 | tf_op jit(solution)/shard_map/convert_element_type | solution.py:31
  254.7 151.0 %all-reduce.6.cloned.1.call-done = f32[768,5632]{1,0:T(8,128)} async-done(((f32[768,5632]{1,0:T(8,128)}), f32[768,5632]{1,0:T(8,128)}) %all-reduce.6.cloned.1.call-update) | async-done | bytes 17301520 | tf_op jit(solution)/shard_map/psum | solution.py:55
  405.7 11.8 %copy.14 = f32[768,5632]{1,0:T(8,128)} copy(f32[768,5632]{1,0:T(8,128)} %all-reduce.6.cloned.1.call-done) | data formatting | bytes 34603008
  (9 shorter events, 0.1 us)
Async XLA Ops:
  7.2 172.3 %all-reduce.4.cloned.1.call-start = ((), (), s32[]{:S(2)}) async-start(), calls=%async_computation | async-start | bytes 3145728 | tf_op jit(solution)/shard_map/psum | solution.py:58
  37.3 14.8 %copy-start.1 = (f32[768]{0:T(1024)S(1)}, f32[768]{0:T(1024)}, u32[]{:S(2)}) copy-start(f32[768]{0:T(1024)} %param.8) | copy-start | bytes 9220
  37.3 14.8 %copy-start.4 = (f32[5632]{0:T(1024)S(1)}, f32[5632]{0:T(1024)}, u32[]{:S(2)}) copy-start(f32[5632]{0:T(1024)} %param.10) | copy-start | bytes 67588
  52.2 24.6 %copy-start.3 = (s32[512]{0:T(512)S(1)}, s32[512]{0:T(512)}, u32[]{:S(2)}) copy-start(s32[512]{0:T(512)} %param.11) | copy-start | bytes 6148
  100.0 2.5 copy-start
  110.8 294.9 %all-reduce.6.cloned.1.call-start = ((), (), s32[]{:S(2)}) async-start(), calls=%async_computation.1 | async-start | bytes 34603008 | tf_op jit(solution)/shard_map/psum | solution.py:55
  122.3 57.1 %copy-start.2 = (f32[768]{0:T(1024)S(1)}, f32[768]{0:T(1024)}, u32[]{:S(2)}) copy-start(f32[768]{0:T(1024)} %param.7) | copy-start | bytes 9220
Sparse Core Ops, SparseCore 0:
  111.0 68.4 all-reduce.3
  183.8 221.8 all-reduce.5
where the time goes:
time: 426 us; the launch traced here: 425 us
  waiting for transfers between devices  208 us (49%)
  other arithmetic  109 us (26%)
  blocking collectives  47.7 us (11%)
  matrix products  30.8 us (7%)
  between operations  16 us (4%)
  local copies, waits for them, and re-layouts  14.3 us (3%)
    psum x1, waiting for transfers between devices, local_head(): lax.psum(lax.dot_general(pooled16, dlogit16, (((0,), (0,)), ((), ())), pr...  151 us
    psum x1, waiting for transfers between devices, local_head(): grad_pool = lax.psum(grad_pool, 'tp')  56.5 us
    convert_element_type x1, other arithmetic, norm_backward(): return (grad_x.astype(jnp.bfloat16), grad_gamma, grad_beta)  26.2 us
    psum x1, blocking collectives, local_head(): lax.psum((jnp.sum(loss_rows), grad_gamma, grad_beta), 'dp')  25.7 us
    reduce_sum x1, other arithmetic, norm_backward(): proj_term = jnp.mean(x_hat * upstream[:, None, :], axis=-1, keepdims=True)  20.5 us
    reduce_sum x1, other arithmetic, norm_pool(): var_x = jnp.mean(centered * centered, axis=-1, keepdims=True)  16.7 us
    reduce_sum x1, other arithmetic, norm_pool(): x_hat_mean = jnp.mean(x_hat, axis=1)  14.8 us
    unnamed x11, local copies, waits for them, and re-layouts  14.3 us
  transfers between devices with their start and end apart: 2, of which 2 were waited for; matrix products, arithmetic and copies ran while one was open for 14% of the time, Pallas kernels for 0%

commit v1 on v0

v1 whole, which is shorter than its diff:
```python
import functools
import jax
import jax.numpy as jnp
from jax import lax
from jax.experimental import pallas as pl
from jax.experimental.pallas import tpu as pltpu
from jax.sharding import PartitionSpec as P

VALID_CLASSES = 21841
LN_EPS = 1e-5
SMOOTH = 0.1
BATCH = 4096
TOKENS = 49
WIDTH = 768
HALF = 2816
TILE = 256
NT = HALF // TILE
NPLAIN = 8
RB = 256
NB = BATCH // RB
ROWS = 512
SUB = 32
PROWS = WIDTH + 8
ARC = 6
VMEM_ALL = 64 * 1024 * 1024 - 65536
F32 = jnp.float32
BF16 = jnp.bfloat16


def coords():
    z = lax.axis_index("tp")
    dp = lax.axis_index("dp")
    c = lax.rem(dp, 2)
    x = lax.rem(dp // 2, 2)
    y = dp // 4
    return z, dp, y, x, c


def ln_gather_kernel(f_hbm, lab_ref, gam_ref, bet_ref, pall, xhm_ref, stat_ref,
                     fbuf, pbuf, psend, fsem, loc, sx, sy, sc, rx, ry, rc):
    z, dp, y, x, c = coords()
    dpx = dp + 2 - 4 * x
    dpy = dp + 4 - 8 * y
    dpc = dp + 1 - 2 * c
    dpd = dpx + 4 - 8 * y

    bar = pltpu.get_barrier_semaphore()
    for d in (dpx, dpy, dpc):
        pl.semaphore_signal(bar, inc=1, device_id={"dp": d}, device_id_type=pl.DeviceIdType.MESH)

    def load(i, slot):
        return pltpu.make_async_copy(f_hbm.at[:, pl.ds(pl.multiple_of(i * SUB, SUB), SUB), :], fbuf.at[slot], fsem.at[slot])

    def rcopy(src, chunk, ss, rs, dev):
        return pltpu.make_async_remote_copy(src_ref=src, dst_ref=pall.at[chunk], send_sem=ss, recv_sem=rs,
                                            device_id={"dp": dev}, device_id_type=pl.DeviceIdType.MESH)

    load(0, 0).start()
    lane = lax.broadcasted_iota(jnp.int32, (16, 128), 1)

    def sub_step(k, s, carry):
        i = k * 4 + s
        slot = lax.rem(i, 2)

        @pl.when(i + 1 < ROWS // SUB)
        def _():
            load(i + 1, 1 - slot).start()

        load(i, slot).wait()
        for rt in range(SUB // 16):
            row = pl.multiple_of(i * SUB + rt * 16, 16)

            def group(g, acc):
                st = jnp.zeros((16, 128), F32)
                for j in range(7):
                    v = fbuf[slot, g * 7 + j, rt * 16:rt * 16 + 16, :].astype(F32)
                    m = jnp.sum(v, axis=-1, keepdims=True) * (1.0 / WIDTH)
                    cv = v - m
                    inv = lax.rsqrt(jnp.sum(cv * cv, axis=-1, keepdims=True) * (1.0 / WIDTH) + LN_EPS)
                    acc = acc + cv * inv
                    st = jnp.where(lane == j, m, jnp.where(lane == 64 + j, inv, st))
                stat_ref[g, pl.ds(row, 16), :] = st
                return acc

            acc = lax.fori_loop(0, 7, group, jnp.zeros((16, WIDTH), F32))
            xh = acc * (1.0 / TOKENS)
            xhm_ref[pl.ds(row, 16), :] = xh
            pv = (xh * gam_ref[...] + bet_ref[...]).astype(BF16).astype(F32)
            pbuf[pl.ds(pl.multiple_of(s * SUB + rt * 16, 16), 16), :] = pv
        return carry

    sends = []
    locals_ = []
    for k in range(4):
        lax.fori_loop(0, 4, functools.partial(sub_step, k), 0)
        psend[k, 0:WIDTH, :] = pbuf[...].T
        psend[k, WIDTH:PROWS, :] = jnp.broadcast_to(lab_ref[k], (8, 128))
        if k == 0:
            pl.semaphore_wait(bar, 3)
        ch = dp * 4 + k
        for cp in (rcopy(psend.at[k], ch, sx.at[k], rx.at[k], dpx),
                   rcopy(psend.at[k], ch, sy.at[k], ry.at[k], dpy),
                   rcopy(psend.at[k], ch, sc.at[k], rc.at[k], dpc)):
            cp.start()
            sends.append(cp)
        lc = pltpu.make_async_copy(psend.at[k], pall.at[ch], loc.at[k])
        lc.start()
        locals_.append(lc)

    def relay(chunk, ss, rs, dev):
        cp = rcopy(pall.at[chunk], chunk, ss, rs, dev)
        cp.start()
        sends.append(cp)

    for k in range(4):
        cx = dpx * 4 + k
        rcopy(pall.at[cx], cx, sx.at[k], rx.at[k], dpx).wait_recv()
        if k < 2:
            relay(cx, sy.at[4 + k], ry.at[4 + k], dpy)
        relay(cx, sc.at[4 + k], rc.at[4 + k], dpc)
        cy = dpy * 4 + k
        rcopy(pall.at[cy], cy, sy.at[k], ry.at[k], dpy).wait_recv()
        if k >= 2:
            relay(cy, sx.at[2 + k], rx.at[2 + k], dpx)
        relay(cy, sc.at[8 + k], rc.at[8 + k], dpc)
    for k in range(4):
        cd = dpd * 4 + k
        if k < 2:
            rcopy(pall.at[cd], cd, sy.at[4 + k], ry.at[4 + k], dpy).wait_recv()
        else:
            rcopy(pall.at[cd], cd, sx.at[2 + k], rx.at[2 + k], dpx).wait_recv()
        relay(cd, sc.at[12 + k], rc.at[12 + k], dpc)
    for q, d in enumerate((dp, dpx, dpy, dpd)):
        for k in range(4):
            ch = (d + 1 - 2 * c) * 4 + k
            rcopy(pall.at[ch], ch, sc.at[q * 4 + k], rc.at[q * 4 + k], dpc).wait_recv()
    for cp in sends:
        cp.wait_send()
    for cp in locals_:
        cp.wait()


def ln_gather(f_t, lab, gam, bet):
    dma = pltpu.SemaphoreType.DMA
    vm = pl.BlockSpec(memory_space=pltpu.VMEM)
    hbm = pl.BlockSpec(memory_space=pl.ANY)
    return pl.pallas_call(
        ln_gather_kernel,
        out_shape=(jax.ShapeDtypeStruct((BATCH // 128, PROWS, 128), F32),
                   jax.ShapeDtypeStruct((ROWS, WIDTH), F32),
                   jax.ShapeDtypeStruct((7, ROWS, 128), F32)),
        in_specs=[hbm, vm, vm, vm],
        out_specs=(hbm, vm, vm),
        scratch_shapes=[pltpu.VMEM((2, TOKENS, SUB, WIDTH), BF16), pltpu.VMEM((128, WIDTH), F32),
                        pltpu.VMEM((4, PROWS, 128), F32), dma((2,)), dma((4,)),
                        dma((6,)), dma((6,)), dma((16,)), dma((6,)), dma((6,)), dma((16,))],
        compiler_params=pltpu.CompilerParams(collective_id=0, has_side_effects=True, vmem_limit_bytes=VMEM_ALL),
        name="ln_gather",
    )(f_t, lab, gam, bet)


def head_kernel(pall, wt_ref, w_hbm, b_ref, iota_ref, dpool_ref, dwo, dwr, db_ref, dbr, loss_ref,
                dlt, ering, ptb, pbuf, ylab, sbuf, dpa, d2d, ubuf, dbuf, dsend, dwt,
                psem, wsem, ss, rs, cs, cr, us, ur, ds_, dr, dls, dss, dsr, bs, br):
    z, dp, y, x, c = coords()
    dpc = dp + 1 - 2 * c
    me = z * 2 + c
    MESH = pl.DeviceIdType.MESH
    colbase = (z * 2 + c) * HALF
    colbase_f = colbase.astype(F32)
    limit_f = (VALID_CLASSES - colbase).astype(F32)

    bar = pltpu.get_barrier_semaphore()
    for j in range(7):
        p = lax.rem(me + 1 + j, 8)
        pl.semaphore_signal(bar, inc=1, device_id={"tp": p // 2, "dp": dp - c + lax.rem(p, 2)}, device_id_type=MESH)

    wcopy = pltpu.make_async_copy(w_hbm, dlt.at[0:WIDTH, 1024:1024 + HALF], wsem)
    wcopy.start()

    def chunk_of(r, h):
        q = r // 2
        qc = q // 2
        gx = lax.rem(x + lax.rem(qc, 2), 2)
        gy = lax.rem(y + qc // 2, 2)
        return (gy * 4 + gx * 2 + lax.rem(q, 2)) * 4 + lax.rem(r, 2) * 2 + h

    def ploads(r):
        slot = lax.rem(r, 2)
        return [pltpu.make_async_copy(pall.at[chunk_of(r, h)], pbuf.at[slot, h], psem.at[slot, h]) for h in range(2)]

    for cp in ploads(0):
        cp.start()
    db_ref[...] = jnp.zeros_like(db_ref)
    loss_ref[...] = jnp.zeros_like(loss_ref)
    pl.semaphore_wait(bar, 7)

    def ci():
        v = iota_ref[...]
        return jnp.concatenate([v, v], axis=1)

    def fwd_block(r):
        slot = lax.rem(r, 2)

        @pl.when(r + 1 < NB)
        def _():
            for cp in ploads(r + 1):
                cp.start()

        for cp in ploads(r):
            cp.wait()
        pb = jnp.concatenate([pbuf[slot, 0, 0:WIDTH, :], pbuf[slot, 1, 0:WIDTH, :]], axis=1).astype(BF16)
        lanes = pl.ds(pl.multiple_of(r * RB, RB), RB)
        ptb[:, lanes] = pb
        yb = jnp.concatenate([pbuf[slot, 0, WIDTH:PROWS, :], pbuf[slot, 1, WIDTH:PROWS, :]], axis=1) - colbase_f
        ylab[r] = yb
        es = lax.rem(r, 4)

        def pass1(n, masked, carry):
            mx, tg, vs = carry
            rows = pl.ds(pl.multiple_of(n * TILE, TILE), TILE)
            bb = b_ref[rows, :]
            l = jnp.dot(wt_ref[rows, :], ptb[:, lanes], preferred_element_type=F32) + jnp.concatenate([bb, bb], axis=1)
            off = lax.convert_element_type(n * TILE, F32)
            yy = jnp.broadcast_to((yb - off)[None], (TILE // 8, 8, RB)).reshape(TILE, RB)
            hot = ci() == yy
            tg = tg + jnp.where(hot, l, 0.0).reshape(TILE // 8, 8, RB).sum(axis=0)
            vs = vs + l.reshape(TILE // 8, 8, RB).sum(axis=0)
            if masked:
                l = jnp.where(ci() < limit_f - off, l, -1e30)
            ering[es, rows, :] = l
            mx = jnp.maximum(mx, l.reshape(TILE // 8, 8, RB).max(axis=0))
            return mx, tg, vs

        zero = jnp.zeros((8, RB), F32)
        carry = (jnp.full((8, RB), -3e38, F32), zero, zero)
        carry = lax.fori_loop(0, NPLAIN, lambda n, cr_: pass1(n, False, cr_), carry)
        carry = lax.fori_loop(NPLAIN, NT, lambda n, cr_: pass1(n, True, cr_), carry)
        mx, tg, vs = carry
        m = jnp.max(mx, axis=0, keepdims=True)
        mb = jnp.broadcast_to(m, (TILE, RB))

        def pass2(n, s):
            rows = pl.ds(pl.multiple_of(n * TILE, TILE), TILE)
            e = jnp.exp(ering[es, rows, :] - mb)
            ering[es, rows, :] = e
            return s + e.reshape(TILE // 8, 8, RB).sum(axis=0)

        s = lax.fori_loop(0, NT, pass2, zero)
        sbuf[r, 7, 0:1, :] = m
        sbuf[r, 7, 1:2, :] = jnp.sum(s, axis=0, keepdims=True)
        sbuf[r, 7, 2:3, :] = jnp.sum(tg, axis=0, keepdims=True)
        sbuf[r, 7, 3:4, :] = jnp.sum(vs, axis=0, keepdims=True)
        for j in range(7):
            p = lax.rem(me + 1 + j, 8)
            pltpu.make_async_remote_copy(
                src_ref=sbuf.at[r, 7], dst_ref=sbuf.at[r, 6 - j], send_sem=ss.at[r, j], recv_sem=rs.at[r, 6 - j],
                device_id={"tp": p // 2, "dp": dp - c + lax.rem(p, 2)}, device_id_type=MESH).start()

    c0 = (SMOOTH / VALID_CLASSES) / BATCH
    c1 = c0 + (1.0 - SMOOTH) / BATCH

    def dl_block(r):
        es = lax.rem(r, 4)
        for j in range(7):
            p = lax.rem(me + 1 + j, 8)
            cp = pltpu.make_async_remote_copy(
                src_ref=sbuf.at[r, 7], dst_ref=sbuf.at[r, j], send_sem=ss.at[r, j], recv_sem=rs.at[r, j],
                device_id={"tp": p // 2, "dp": dp - c + lax.rem(p, 2)}, device_id_type=MESH)
            cp.wait_recv()
            cp.wait_send()
        mown = sbuf[r, 7, 0:1, :]
        gm = mown
        for j in range(7):
            gm = jnp.maximum(gm, sbuf[r, j, 0:1, :])
        zs = jnp.zeros_like(gm)
        ts = jnp.zeros_like(gm)
        vs = jnp.zeros_like(gm)
        for j in range(8):
            zs = zs + sbuf[r, j, 1:2, :] * jnp.exp(sbuf[r, j, 0:1, :] - gm)
            ts = ts + sbuf[r, j, 2:3, :]
            vs = vs + sbuf[r, j, 3:4, :]
        loss_ref[...] += gm + jnp.log(zs) - (1.0 - SMOOTH) * ts - (SMOOTH / VALID_CLASSES) * vs
        scale = jnp.exp(mown - gm) / (zs * BATCH)
        scb = jnp.broadcast_to(scale, (TILE, RB))
        yb = ylab[r]
        lanes = pl.ds(pl.multiple_of(r * RB, RB), RB)

        def tile(n, masked):
            rows = pl.ds(pl.multiple_of(n * TILE, TILE), TILE)
            off = lax.convert_element_type(n * TILE, F32)
            yy = jnp.broadcast_to((yb - off)[None], (TILE // 8, 8, RB)).reshape(TILE, RB)
            hot = ci() == yy
            base = jnp.where(ci() < limit_f - off, c0, 0.0) if masked else c0
            d = ering[es, rows, :] * scb - jnp.where(hot, c1, base)
            db_ref[rows, :] += d[:, 0:128] + d[:, 128:256]
            dlt[rows, lanes] = d.astype(BF16)

        def plain(n, cr_):
            tile(n, False)
            return cr_

        def mask(n, cr_):
            tile(n, True)
            return cr_

        lax.fori_loop(0, NPLAIN, plain, 0)
        lax.fori_loop(NPLAIN, NT, mask, 0)

    def own_fwd(r, cr_):
        fwd_block(r)
        return cr_

    def own_dl(r, cr_):
        dl_block(r)
        return cr_

    lax.fori_loop(0, 4, own_fwd, 0)
    lax.fori_loop(0, 4, own_dl, 0)
    wcopy.wait()

    def dpool_block(i, cr_):
        lanes = pl.ds(pl.multiple_of(i * RB, RB), RB)
        dpa[i] = jnp.dot(dlt[0:WIDTH, 1024:1024 + HALF], dlt[:, lanes], preferred_element_type=F32)
        return cr_

    lax.fori_loop(0, 4, dpool_block, 0)
    d2c = pltpu.make_async_remote_copy(
        src_ref=dpa.at[pl.ds((1 - c) * 2, 2)], dst_ref=d2d, send_sem=cs, recv_sem=cr,
        device_id={"dp": dpc}, device_id_type=MESH)
    d2c.start()
    d2c.wait()
    for h in range(2):
        d2d[h] = d2d[h] + dpa[c * 2 + h]

    def own(j):
        rows = pl.ds(pl.multiple_of(j * 128, 128), 128)
        return jnp.concatenate([d2d[0, rows, :], d2d[1, rows, :]], axis=1)

    def up(j):
        return pltpu.make_async_remote_copy(src_ref=ubuf.at[j], dst_ref=ubuf.at[j], send_sem=us.at[j], recv_sem=ur.at[j],
                                            device_id={"tp": jnp.minimum(z + 1, 3)}, device_id_type=MESH)

    def down(j):
        return pltpu.make_async_remote_copy(src_ref=dsend.at[j], dst_ref=dbuf.at[j], send_sem=ds_.at[j], recv_sem=dr.at[j],
                                            device_id={"tp": jnp.maximum(z - 1, 0)}, device_id_type=MESH)

    @pl.when(z == 0)
    def _():
        for j in range(ARC):
            ubuf[j] = own(j)
            up(j).start()

    @pl.when(z == 3)
    def _():
        for j in range(ARC):
            dsend[j] = own(j)
            down(j).start()

    def tick(t):
        tu = t - 3 * z - 1

        @pl.when((z >= 1) & (tu >= 0) & (lax.rem(tu, 2) == 0) & (tu // 2 < ARC))
        def _():
            j = tu // 2
            up(j).wait_recv()
            ubuf[j] = ubuf[j] + own(j)

            @pl.when(z < 3)
            def _():
                up(j).start()

        td = t - 3 * (3 - z) - 1

        @pl.when((z <= 2) & (td >= 0) & (lax.rem(td, 2) == 0) & (td // 2 < ARC))
        def _():
            j = td // 2
            down(j).wait_recv()

            @pl.when(z > 0)
            def _():
                dsend[j] = dbuf[j] + own(j)
                down(j).start()

    def rest(r, cr_):
        fwd_block(r)

        @pl.when(r >= 6)
        def _():
            dl_block(r - 2)

        tick(r - 4)
        return cr_

    lax.fori_loop(4, NB, rest, 0)
    lax.fori_loop(NB - 2, NB, own_dl, 0)

    dbc = pltpu.make_async_remote_copy(src_ref=db_ref, dst_ref=dbr, send_sem=bs, recv_sem=br,
                                       device_id={"dp": dpc}, device_id_type=MESH)
    dbc.start()

    def dw_local(n):
        slot = lax.rem(n, 2)
        return pltpu.make_async_copy(dwt.at[slot], dwo.at[:, pl.ds(pl.multiple_of(n * TILE, TILE), TILE)], dls.at[slot])

    def dw_remote(n):
        slot = lax.rem(n, 2)
        return pltpu.make_async_remote_copy(
            src_ref=dwt.at[slot], dst_ref=dwr.at[:, pl.ds(pl.multiple_of(n * TILE, TILE), TILE)],
            send_sem=dss.at[slot], recv_sem=dsr.at[n], device_id={"dp": dpc}, device_id_type=MESH)

    def dw_step(n, cr_):
        @pl.when(n >= 2)
        def _():
            dw_local(n - 2).wait()
            dw_remote(n - 2).wait_send()

        rows = pl.ds(pl.multiple_of(n * TILE, TILE), TILE)
        dwt[lax.rem(n, 2)] = lax.dot_general(ptb[...], dlt[rows, :], (((1,), (1,)), ((), ())), preferred_element_type=F32)
        dw_local(n).start()
        dw_remote(n).start()
        tick(n + 12)
        return cr_

    lax.fori_loop(0, NT, dw_step, 0)

    for j in range(ARC):
        tot = jnp.where(z < 3, dbuf[j], 0.0) + ubuf[j]
        dpool_ref[:, j * 128:(j + 1) * 128] = tot.T

    for n in (NT - 2, NT - 1):
        dw_local(n).wait()
        dw_remote(n).wait_send()

    def dw_recv(n, cr_):
        dw_remote(n).wait_recv()
        return cr_

    lax.fori_loop(0, NT, dw_recv, 0)
    dbc.wait()

    @pl.when(z < 3)
    def _():
        for j in range(ARC):
            up(j).wait_send()

    @pl.when(z > 0)
    def _():
        for j in range(ARC):
            down(j).wait_send()


def head(pall, wt, w, bb, iota):
    dma = pltpu.SemaphoreType.DMA
    vm = pl.BlockSpec(memory_space=pltpu.VMEM)
    hbm = pl.BlockSpec(memory_space=pl.ANY)
    V = pltpu.VMEM
    return pl.pallas_call(
        head_kernel,
        out_shape=(jax.ShapeDtypeStruct((ROWS, WIDTH), F32),
                   jax.ShapeDtypeStruct((WIDTH, HALF), F32),
                   jax.ShapeDtypeStruct((WIDTH, HALF), F32),
                   jax.ShapeDtypeStruct((HALF, 128), F32),
                   jax.ShapeDtypeStruct((HALF, 128), F32),
                   jax.ShapeDtypeStruct((1, RB), F32)),
        in_specs=[hbm, vm, hbm, vm, vm],
        out_specs=(vm, hbm, hbm, vm, hbm, vm),
        scratch_shapes=[V((HALF, BATCH), BF16), V((4, HALF, RB), F32), V((WIDTH, BATCH), BF16),
                        V((2, 2, PROWS, 128), F32), V((NB, 8, RB), F32), V((NB, 8, 4, RB), F32),
                        V((4, WIDTH, RB), F32), V((2, WIDTH, RB), F32),
                        V((ARC, 128, ROWS), F32), V((ARC, 128, ROWS), F32), V((ARC, 128, ROWS), F32),
                        V((2, WIDTH, TILE), F32),
                        dma((2, 2)), dma, dma((NB, 7)), dma((NB, 7)), dma, dma,
                        dma((ARC,)), dma((ARC,)), dma((ARC,)), dma((ARC,)),
                        dma((2,)), dma((2,)), dma((NT,)), dma, dma],
        compiler_params=pltpu.CompilerParams(collective_id=1, has_side_effects=True, vmem_limit_bytes=VMEM_ALL),
        name="head",
    )(pall, wt, w, bb, iota)


def ln_bwd_kernel(f_ref, stat_ref, dp_ref, gam_ref, o_ref):
    for rt in range(SUB // 16):
        rs = slice(rt * 16, rt * 16 + 16)
        u = dp_ref[rs, :] * gam_ref[...] * (1.0 / TOKENS)
        u = u - jnp.sum(u, axis=-1, keepdims=True) * (1.0 / WIDTH)

        def group(g, cr_):
            st = stat_ref[g, rs, :]
            for j in range(7):
                m = st[:, j:j + 1]
                inv = st[:, 64 + j:65 + j]
                d = f_ref[g * 7 + j, rs, :].astype(F32) - m
                pr = jnp.sum(d * u, axis=-1, keepdims=True) * (1.0 / WIDTH)
                o_ref[g * 7 + j, rs, :] = (inv * u - (inv * inv * inv * pr) * d).astype(BF16)
            return cr_

        lax.fori_loop(0, 7, group, 0)


def ln_bwd(f_t, stat, dpool, gam):
    blk = pl.BlockSpec((TOKENS, SUB, WIDTH), lambda i: (0, i, 0))
    return pl.pallas_call(
        ln_bwd_kernel,
        grid=(ROWS // SUB,),
        out_shape=jax.ShapeDtypeStruct((TOKENS, ROWS, WIDTH), BF16),
        in_specs=[blk, pl.BlockSpec((7, SUB, 128), lambda i: (0, i, 0)),
                  pl.BlockSpec((SUB, WIDTH), lambda i: (i, 0)), pl.BlockSpec((1, WIDTH), lambda i: (0, 0))],
        out_specs=blk,
        name="ln_bwd",
    )(f_t, stat, dpool, gam)


def solution(mesh):
    def local(feats, gamma, beta, w, b, labels):
        z, dp, y, x, c = coords()
        f_t = jnp.transpose(feats, (1, 0, 2))
        lab = labels.astype(F32).reshape(4, 1, 128)
        col = (z * 2 + c) * HALF + jnp.arange(HALF)
        valid = col < VALID_CLASSES
        wh = jnp.where(valid[None, :], lax.dynamic_slice(w, (0, c * HALF), (WIDTH, HALF)), jnp.zeros((), BF16))
        bh = jnp.where(valid, lax.dynamic_slice(b, (c * HALF,), (HALF,)), 0.0)
        bb = jnp.broadcast_to(bh[:, None], (HALF, 128))
        iota = lax.broadcasted_iota(F32, (TILE, 128), 0)
        pall, xhm, stat = ln_gather(f_t, lab, gamma[None, :], beta[None, :])
        dpool, dwo, dwr, dbo, dbr, loss = head(pall, wh.T, wh, bb, iota)
        df_t = ln_bwd(f_t, stat, dpool, gamma[None, :])
        gsum = lax.psum(jnp.stack([jnp.sum(dpool * xhm, axis=0), jnp.sum(dpool, axis=0)]), "dp")
        dw = jnp.concatenate([jnp.where(c == 0, dwo, dwr), jnp.where(c == 0, dwr, dwo)], axis=1)
        dbs = jnp.sum(dbo, axis=1)
        dbrs = jnp.sum(dbr, axis=1)
        db = jnp.concatenate([jnp.where(c == 0, dbs, dbrs), jnp.where(c == 0, dbrs, dbs)])
        return jnp.sum(loss) / BATCH, jnp.transpose(df_t, (1, 0, 2)), dw, db, gsum[0], gsum[1]

    return jax.shard_map(local, mesh=mesh, in_specs=(P("dp", None, None), P(), P(), P(None, "tp"), P("tp"), P("dp")),
                         out_specs=(P(), P("dp", None, None), P(None, "tp"), P("tp"), P(), P()), check_vma=False)
```

time: 426 us -> 394 us (0.925)
  Pallas kernels: 0 us -> 334 us
  waiting for transfers between devices: 208 us -> 0 us
  other arithmetic: 109 us -> 31.6 us
  blocking collectives: 47.7 us -> 13.4 us
  matrix products: 30.8 us -> 0 us
  between operations: 16 us -> 2.52 us
    pallas_call x0 -> x3, Pallas kernels: none -> 334 us  [the longest x1 151 us: head(): pl.pallas_call(head_kernel, out_shape=(jax.ShapeDtypeStruct((ROWS, WIDTH)...]
    psum x2 -> x0, waiting for transfers between devices: 208 us -> none  [the longest x1 151 us: local_head(): lax.psum(lax.dot_general(pooled16, dlogit16, (((0,), (0,)), ((), ())), pr...]
    reduce_sum x8 -> x4, other arithmetic: 81.8 us -> 5.69 us  [the longest x1 2.21 us: local(): jnp.sum(dpool * xhm, axis=0)]
    dot_general x3 -> x0, matrix products: 30.8 us -> none  [the longest x1 11.4 us: local_head(): lax.dot_general(pooled16, dlogit16, (((0,), (0,)), ((), ())), preferred_e...]
    convert_element_type x1, other arithmetic: 26.2 us -> 1.26 us  [local(): lab = labels.astype(F32).reshape(4, 1, 128)]
    psum x2 -> x1, blocking collectives: 34.3 us -> 13.4 us  [local(): lax.psum(jnp.stack([jnp.sum(dpool * xhm, axis=0), jnp.sum(dpool, axis=0)]...]
    unnamed x11 -> x2, local copies, waits for them, and re-layouts: 14.3 us -> 0.01 us
    pmax x1 -> x0, blocking collectives: 13.5 us -> none  [local_head(): row_max = lax.pmax(jnp.max(logits, axis=-1), 'tp')]
  transfers between devices with their start and end apart: 2 -> 0, of which waited for: 2 -> 0; matrix products, arithmetic and copies ran while one was open for 14% -> 0% of each run, Pallas kernels for 0% -> 0%
where the time goes in v1:
time: 394 us; the launch traced here: 393 us
  Pallas kernels  334 us (85%)
  other arithmetic  31.6 us (8%)
  blocking collectives  13.4 us (3%)
  local copies, waits for them, and re-layouts  11.8 us (3%)
    pallas_call x1, Pallas kernels, head(): pl.pallas_call(head_kernel, out_shape=(jax.ShapeDtypeStruct((ROWS, WIDTH)...  151 us
    pallas_call x1, Pallas kernels, ln_bwd(): pl.pallas_call(ln_bwd_kernel, grid=(ROWS // SUB,), out_shape=jax.ShapeDty...  96.2 us
    pallas_call x1, Pallas kernels, ln_gather(): pl.pallas_call(ln_gather_kernel, out_shape=(jax.ShapeDtypeStruct((BATCH /...  86.8 us
    psum x1, blocking collectives, local(): lax.psum(jnp.stack([jnp.sum(dpool * xhm, axis=0), jnp.sum(dpool, axis=0)]...  13.4 us

profile of v1, /device:TPU:0, one launch (start us, length us, event | category | flops | bytes accessed | tf_op | source)
XLA Modules:
  0.0 393.2 jit_solution(16958489920831298335)
XLA Ops:
  0.6 1.3 convert_element_type.3
  1.9 1.3 broadcast_in_dim.30.gam_ref
  3.2 1.3 broadcast_in_dim.31.bet_ref
  4.5 0.8 dynamic-slice_select_fusion.1
  5.3 0.7 iota.11.iota_ref
  5.9 1.5 broadcast_in_dim.35.b_ref
  7.5 5.0 %fusion = bf16[2816,768]{0,1:T(8,128)(2,1)} fusion(bf16[768,5632]{1,0:T(8,128)(2,1)} %param.9, s32[]{:T(128)S(6)} %select_n.36, pred[2816]{0:T(1024)(128)(4,1)S(1)} %add_compare_fusion), kind=kLoop, calls=%fused_computation.13 | loop fusion | flops 2162688 | bytes 8653572 | tf_op jit(solution)/shard_map/transpose | solution.py:525
  12.5 6.4 %copy.12.wt_ref = bf16[2816,768]{1,0:T(8,128)(2,1)} copy(bf16[2816,768]{0,1:T(8,128)(2,1)} %fusion) | data formatting | bytes 8650752 | tf_op jit(solution)/shard_map/transpose | solution.py:525
  18.9 5.0 %dynamic-slice_select_fusion.w_hbm = bf16[768,2816]{1,0:T(8,128)(2,1)} fusion(bf16[768,5632]{1,0:T(8,128)(2,1)} %param.9, s32[]{:T(128)S(6)} %select_n.36, pred[2816]{0:T(1024)(128)(4,1)S(1)} %add_compare_fusion), kind=kLoop, calls=%fused_computation.1 | loop fusion | flops 2162688 | bytes 8653572 | tf_op jit(solution)/shard_map/jit(_where)/select_n | solution.py:520
  24.0 86.8 %ln_gather.1 = (f32[32,776,128]{2,1,0:T(8,128)}, f32[512,768]{1,0:T(8,128)}, f32[7,512,128]{2,1,0:T(8,128)}) custom-call(bf16[49,512,768]{2,1,0:T(8,128)(2,1)} %bitcast.5, f32[4,1,128]{2,1,0:T(1,128)} %bitcast.8, f32[1,768]{1,0:T(1,128)} %broadcast_in_dim.30.gam_ref, f32[1,768]{1,0:T(1,128)} %broadcast_in_dim.31.bet_ref), custom_call_target="tpu_custom_call" | custom-call | tf_op jit(solution)/shard_map/ln_gather/pallas_call | solution.py:147
  110.7 150.9 %head.1 = (f32[512,768]{1,0:T(8,128)}, f32[768,2816]{1,0:T(8,128)}, f32[768,2816]{1,0:T(8,128)}, f32[2816,128]{1,0:T(8,128)}, f32[2816,128]{1,0:T(8,128)}, /*index=5*/f32[1,256]{1,0:T(1,128)}) custom-call(f32[32,776,128]{2,1,0:T(8,128)} %get-tuple-element.15.pall, bf16[2816,768]{1,0:T(8,128)(2,1)} %copy.12.wt_ref, ...), custom_call_target="tpu_custom_call" | custom-call | tf_op jit(solution)/shard_map/head/pallas_call | solution.py:458
  261.6 0.0 copy-start
  261.6 2.2 multiply_reduce_fusion
  263.8 1.2 reduce_sum.45
  265.7 13.4 %psum.7 = f32[2,768]{1,0:T(2,128)S(1)} all-reduce(f32[2,768]{1,0:T(2,128)S(1)} %pad_maximum_fusion.2), channel_id=1, replica_groups=mesh['tp'=4,'dp'=8] {'dp'}, use_global_device_ids=true, to_apply=%region_5.6 | all-reduce | flops 1536 | bytes 12288 | tf_op jit(solution)/shard_map/psum | solution.py:527
  279.1 0.6 slice_reduce_fusion
  279.7 1.8 reduce_sum.46
  281.6 0.0 copy-done
  281.6 0.4 reduce_sum.47
  282.0 6.6 %broadcast_select_fusion.1 = (f32[768,2816]{1,0:T(8,128)S(1)}, f32[768,2816]{1,0:T(8,128)S(1)}) fusion(f32[768,2816]{1,0:T(8,128)} %get-tuple-element.19, f32[768,2816]{1,0:T(8,128)} %get-tuple-element.20, pred[]{:T(512)S(6)} %eq.2), kind=kLoop, calls=%fused_computation.3 | loop fusion | flops 4325376 | bytes 34603008 | tf_op jit(solution)/shard_map/jit(_where)/select_n | solution.py:528
  288.6 6.6 %pad_maximum_fusion = f32[768,5632]{1,0:T(8,128)} fusion(f32[768,2816]{1,0:T(8,128)S(1)} %get-tuple-element.29, f32[768,2816]{1,0:T(8,128)S(1)} %get-tuple-element.28), kind=kLoop, calls=%fused_computation | loop fusion | flops 4325376 | bytes 34603008 | tf_op jit(solution)/shard_map/concatenate | solution.py:528
  295.2 0.6 pad_maximum_fusion.1
  295.8 96.2 %ln_bwd.1 = bf16[49,512,768]{2,1,0:T(8,128)(2,1)} custom-call(bf16[49,512,768]{2,1,0:T(8,128)(2,1)} %bitcast.6, f32[7,512,128]{2,1,0:T(8,128)} %get-tuple-element.17.stat_ref, f32[512,768]{1,0:T(8,128)} %get-tuple-element.18.dp_ref, f32[1,768]{1,0:T(1,128)} %broadcast_in_dim.30.gam_ref), custom_call_target="tpu_custom_call" | custom-call | tf_op jit(solution)/shard_map/ln_bwd/pallas_call | solution.py:502
  (5 shorter events, 0.0 us)
Async XLA Ops:
  261.6 19.9 %copy-start = (f32[2816,128]{1,0:T(8,128)S(1)}, f32[2816,128]{1,0:T(8,128)}, u32[]{:S(2)}) copy-start(f32[2816,128]{1,0:T(8,128)} %get-tuple-element.22) | copy-start | bytes 4325380

commit v2 on v0

v2 whole, which is shorter than its diff:
```python
import functools
import jax
import jax.numpy as jnp
from jax import lax
from jax.experimental import pallas as pl
from jax.experimental.pallas import tpu as pltpu
from jax.sharding import PartitionSpec as P

VALID_CLASSES = 21841
LN_EPS = 1e-5
SMOOTH = 0.1
BATCH = 4096
TOKENS = 49
WIDTH = 768
HALF = 2816
TILE = 256
NT = HALF // TILE
LT = 1408
ET = 704
CLS = 2 * HALF
RB = 256
NB = BATCH // RB
ROWS = 512
SUB = 32
PROWS = WIDTH + 8
ARW = 64
ARC = WIDTH // ARW
LANE = 128
TG = 7
SIDE = 64
PEERS = 7
VMEM_ALL = 64 * 1024 * 1024 - 65536
F32 = jnp.float32
BF16 = jnp.bfloat16


def coords():
    z = lax.axis_index("tp")
    dp = lax.axis_index("dp")
    c = lax.rem(dp, 2)
    x = lax.rem(dp // 2, 2)
    y = dp // 4
    return z, dp, y, x, c


OWN = 4
MESH = pl.DeviceIdType.MESH
C0 = (SMOOTH / VALID_CLASSES) / BATCH
C1 = C0 + (1.0 - SMOOTH) / BATCH


def peer(j):
    z, dp, y, x, c = coords()
    p = lax.rem(z * 2 + c + 1 + j, PEERS + 1)
    return {"tp": p // 2, "dp": dp - c + lax.rem(p, 2)}


def block_code(first, pall, wt_ref, b_ref, loss_ref, dlt, ering, ptb, pbuf, ylab, sbuf, db_ref, iota_ref, psem, ss, rs):
    z, dp, y, x, c = coords()
    colbase = (z * 2 + c) * HALF
    colbase_f = colbase.astype(F32)
    limit_f = (VALID_CLASSES - colbase).astype(F32)
    halves = range(2)

    def chunk_of(r, h):
        q = r // 2
        qc = q // 2
        gx = lax.rem(x + lax.rem(qc, 2), 2)
        gy = lax.rem(y + qc // 2, 2)
        return (gy * 4 + gx * 2 + lax.rem(q, 2)) * 4 + lax.rem(r, 2) * 2 + h

    def ploads(r):
        slot = lax.rem(r, 2)
        return [pltpu.make_async_copy(pall.at[chunk_of(r, h)], pbuf.at[slot, h], psem.at[slot, h]) for h in halves]

    def shifted(yb, off, n):
        return jnp.broadcast_to((yb - off)[None], (n // 8, 8, RB)).reshape(n, RB)

    def ids(n):
        v = iota_ref[0:n, :]
        return jnp.concatenate([v, v], axis=1)

    def fold(v):
        return v.reshape(v.shape[0] // 8, 8, RB)

    def scopy(r, j, slot):
        i = r - first
        return pltpu.make_async_remote_copy(src_ref=sbuf.at[i, PEERS], dst_ref=sbuf.at[i, slot], send_sem=ss.at[i, j],
                                            recv_sem=rs.at[i, slot], device_id=peer(j), device_id_type=MESH)

    def fwd_block(r, stop):
        slot = lax.rem(r, 2)

        @pl.when(r + 1 < stop)
        def _():
            for cp in ploads(r + 1):
                cp.start()

        for cp in ploads(r):
            cp.wait()
        lanes = pl.ds(pl.multiple_of(r * RB, RB), RB)
        ptb[:, lanes] = jnp.concatenate([pbuf[slot, h, 0:WIDTH, :] for h in halves], axis=1).astype(BF16)
        yb = jnp.concatenate([pbuf[slot, h, WIDTH:PROWS, :] for h in halves], axis=1) - colbase_f
        ylab[r - first] = yb
        es = lax.rem(r, OWN)
        zero = jnp.zeros((8, RB), F32)
        mx, tg, vs = jnp.full((8, RB), -3e38, F32), zero, zero
        for n in range(HALF // LT):
            full = jnp.dot(wt_ref[n * LT:(n + 1) * LT, :], ptb[:, lanes], preferred_element_type=F32)
            for lo, size, masked in (((0, LT, 0),) if n == 0 else ((0, ET, 0), (ET, ET, 1))):
                row = n * LT + lo
                bb = b_ref[row:row + size, :]
                l = full[lo:lo + size] + jnp.concatenate([bb, bb], axis=1)
                tg = tg + fold(jnp.where(ids(size) == shifted(yb, float(row), size), l, 0.0)).sum(axis=0)
                if masked:
                    ok = ids(size) < limit_f - float(row)
                    vs = vs + fold(jnp.where(ok, l, 0.0)).sum(axis=0)
                    l = jnp.where(ok, l, -1e30)
                else:
                    vs = vs + fold(l).sum(axis=0)
                ering[es, row:row + size, :] = l
                mx = jnp.maximum(mx, fold(l).max(axis=0))
        m = jnp.max(mx, axis=0, keepdims=True)
        mb = jnp.broadcast_to(m, (ET, RB))

        def pass2(n, s):
            rows = pl.ds(pl.multiple_of(n * ET, ET), ET)
            e = jnp.exp(ering[es, rows, :] - mb)
            ering[es, rows, :] = e
            return s + fold(e).sum(axis=0)

        s = lax.fori_loop(0, HALF // ET, pass2, zero)
        tops = [m] + [jnp.sum(v, axis=0, keepdims=True) for v in (s, tg, vs)]
        for q, v in enumerate(tops):
            sbuf[r - first, PEERS, q:q + 1, :] = v
        for j in range(PEERS):
            scopy(r, j, PEERS - 1 - j).start()

    def dl_block(r):
        es = lax.rem(r, OWN)
        for j in range(PEERS):
            cp = scopy(r, j, j)
            cp.wait_recv()
            cp.wait_send()
        i = r - first
        mown = sbuf[i, PEERS, 0:1, :]
        gm = mown
        for j in range(PEERS):
            gm = jnp.maximum(gm, sbuf[i, j, 0:1, :])
        zs, ts, vs = (jnp.zeros_like(gm) for _ in range(3))
        for j in range(PEERS + 1):
            zs = zs + sbuf[i, j, 1:2, :] * jnp.exp(sbuf[i, j, 0:1, :] - gm)
            ts = ts + sbuf[i, j, 2:3, :]
            vs = vs + sbuf[i, j, 3:4, :]
        loss_ref[...] += gm + jnp.log(zs) - (1.0 - SMOOTH) * ts - (SMOOTH / VALID_CLASSES) * vs
        scb = jnp.broadcast_to(jnp.exp(mown - gm) / (zs * BATCH), (ET, RB))
        yb = ylab[i]
        lanes = pl.ds(pl.multiple_of(r * RB, RB), RB)

        def tile(n, masked):
            rows = pl.ds(pl.multiple_of(n * ET, ET), ET)
            off = lax.convert_element_type(n * ET, F32)
            base = jnp.where(ids(ET) < limit_f - off, C0, 0.0) if masked else C0
            d = ering[es, rows, :] * scb - jnp.where(ids(ET) == shifted(yb, off, ET), C1, base)
            db_ref[rows, :] += d[:, 0:LANE] + d[:, LANE:RB]
            dlt[rows, lanes] = d.astype(BF16)

        def plain(n, cr_):
            tile(n, 0)
            return cr_

        lax.fori_loop(0, HALF // ET - 1, plain, 0)
        tile(HALF // ET - 1, 1)

    return ploads, fwd_block, dl_block


def rep(v):
    return jnp.concatenate([v] * (WIDTH // 128), axis=1)


def ln_gather_kernel(f_hbm, prm, w_hbm, pall, xhm_ref, stat_ref, loss_ref, wt_o, bb_o, dlt_o, ptb_o, db_o, own_o,
                     fbuf, prow, psend, wbuf, mb, ib, ab, wt_ref, bb_ref, dlt, ering, ptb, pbuf, ylab, sbuf, db_ref, iota_ref,
                     dpa, d2d, fsem, wsem, loc, sx, sy, sc, rx, ry, rc, psem, ss, rs, cs, cr, osem):
    z, dp, y, x, c = coords()
    dpx = dp + 2 - 4 * x
    dpy = dp + 4 - 8 * y
    dpc = dp + 1 - 2 * c
    dpd = dpx + 4 - 8 * y

    bar = pltpu.get_barrier_semaphore()
    for d in (dpx, dpy, dpc):
        pl.semaphore_signal(bar, inc=1, device_id={"dp": d}, device_id_type=MESH)
    for j in range(PEERS):
        pl.semaphore_signal(bar, inc=1, device_id=peer(j), device_id_type=MESH)

    def load(i, slot):
        return pltpu.make_async_copy(f_hbm.at[:, pl.ds(pl.multiple_of(i * SUB, SUB), SUB), :], fbuf.at[slot], fsem.at[slot])

    def rcopy(src, chunk, ss, rs, dev):
        return pltpu.make_async_remote_copy(src_ref=src, dst_ref=pall.at[chunk], send_sem=ss, recv_sem=rs,
                                            device_id={"dp": dev}, device_id_type=pl.DeviceIdType.MESH)

    load(0, 0).start()
    half = pl.multiple_of(c * HALF, 128)
    wcopy = pltpu.make_async_copy(w_hbm.at[:, pl.ds(half, HALF)], wbuf, wsem)
    wcopy.start()
    lane = lax.broadcasted_iota(jnp.int32, (SUB, LANE), 1)
    gam = prm[1:2, 0:WIDTH]
    bet = prm[2:3, 0:WIDTH]

    def sub_step(k, s, carry):
        i = k * 4 + s
        slot = lax.rem(i, 2)

        @pl.when(i + 1 < ROWS // SUB)
        def _():
            load(i + 1, 1 - slot).start()

        load(i, slot).wait()
        row = pl.multiple_of(i * SUB, SUB)

        def means(g):
            for j in range(TG):
                v = fbuf[slot, g * TG + j].astype(F32)
                mb[g * TG + j] = jnp.broadcast_to(jnp.sum(v, axis=-1, keepdims=True) * (1.0 / WIDTH), (SUB, LANE))

        def scales(g):
            for j in range(TG):
                t = g * TG + j
                cv = fbuf[slot, t].astype(F32) - rep(mb[t])
                var = jnp.sum(cv * cv, axis=-1, keepdims=True) * (1.0 / WIDTH)
                ib[t] = jnp.broadcast_to(lax.rsqrt(var + LN_EPS), (SUB, LANE))

        def sums(g):
            st = jnp.zeros((SUB, LANE), F32)
            part = jnp.zeros((SUB, WIDTH), F32)
            for j in range(TG):
                t = g * TG + j
                m = mb[t]
                inv = ib[t]
                part = part + (fbuf[slot, t].astype(F32) - rep(m)) * rep(inv)
                st = jnp.where(lane == j, m, jnp.where(lane == SIDE + j, inv, st))
            stat_ref[g, pl.ds(row, SUB), :] = st
            ab[...] += part

        ab[...] = jnp.zeros_like(ab)
        means(0)
        means(1)
        scales(0)

        def body(g, cr_):
            sums(g - 1)
            scales(g)
            means(g + 1)
            return cr_

        lax.fori_loop(1, 6, body, 0)
        sums(5)
        scales(6)
        sums(6)
        xh = ab[...] * (1.0 / TOKENS)
        xhm_ref[pl.ds(row, SUB), :] = xh
        prow[pl.ds(pl.multiple_of(s * SUB, SUB), SUB), :] = (xh * gam + bet).astype(BF16).astype(F32)
        return carry

    sends = []

    def relay(chunk, ss, rs, dev):
        cp = rcopy(pall.at[chunk], chunk, ss, rs, dev)
        cp.start()
        sends.append(cp)

    def pass_on(k):
        cx = dpx * 4 + k
        cy = dpy * 4 + k
        rcopy(pall.at[cx], cx, sx.at[k], rx.at[k], dpx).wait_recv()
        if k % 2 == 0:
            relay(cx, sy.at[4 + k // 2], ry.at[4 + k // 2], dpy)
        relay(cx, sc.at[4 + k], rc.at[4 + k], dpc)
        rcopy(pall.at[cy], cy, sy.at[k], ry.at[k], dpy).wait_recv()
        if k % 2 == 1:
            relay(cy, sx.at[4 + k // 2], rx.at[4 + k // 2], dpx)
        relay(cy, sc.at[8 + k], rc.at[8 + k], dpc)

    locals_ = []
    for k in range(4):
        lax.fori_loop(0, 4, functools.partial(sub_step, k), 0)
        psend[k, 0:WIDTH, :] = prow[...].T
        psend[k, WIDTH:PROWS, :] = jnp.broadcast_to(prm[3:4, k * 128:(k + 1) * 128], (8, 128))
        if k == 0:
            pl.semaphore_wait(bar, 3 + PEERS)
        ch = dp * 4 + k
        for cp in (rcopy(psend.at[k], ch, sx.at[k], rx.at[k], dpx),
                   rcopy(psend.at[k], ch, sy.at[k], ry.at[k], dpy),
                   rcopy(psend.at[k], ch, sc.at[k], rc.at[k], dpc)):
            cp.start()
            sends.append(cp)
        lc = pltpu.make_async_copy(psend.at[k], pall.at[ch], loc.at[k])
        lc.start()
        locals_.append(lc)
        if k >= 2:
            pass_on(k - 2)

    wcopy.wait()

    def turn(n, cr_):
        cols = pl.ds(pl.multiple_of(n * LANE, LANE), 128)
        wt_ref[cols, :] = wbuf[:, cols].T
        bv = prm[0:1, pl.ds(pl.multiple_of(half + n * LANE, LANE), LANE)]
        bb_ref[cols, :] = jnp.broadcast_to(bv, (LANE, LANE)).T
        return cr_

    lax.fori_loop(0, HALF // LANE, turn, 0)

    def out(src, dst, i):
        cp = pltpu.make_async_copy(src, dst, osem.at[i])
        cp.start()
        locals_.append(cp)

    for cp in locals_:
        cp.wait()
    locals_.clear()
    out(wt_ref, wt_o, 0)
    out(bb_ref, bb_o, 1)
    for k in range(4):
        ch = dpc * 4 + k
        rcopy(pall.at[ch], ch, sc.at[k], rc.at[k], dpc).wait_recv()
    pass_on(2)

    ploads, fwd_block, dl_block = block_code(0, pall, wt_ref, bb_ref, loss_ref, dlt, ering, ptb, pbuf, ylab, sbuf, db_ref,
                                             iota_ref, psem, ss, rs)
    iota_ref[...] = lax.broadcasted_iota(jnp.int32, (LT, LANE), 0).astype(F32)
    db_ref[...] = jnp.zeros_like(db_ref)
    loss_ref[...] = jnp.zeros_like(loss_ref)
    for cp in ploads(0):
        cp.start()

    def own_fwd(r, cr_):
        fwd_block(r, OWN)
        return cr_

    def own_dl(r, cr_):
        dl_block(r)
        return cr_

    def dpool_block(i, cr_):
        lanes = pl.ds(pl.multiple_of(i * RB, RB), RB)
        dpa[i] = jnp.dot(wbuf[...], dlt[:, lanes], preferred_element_type=F32)
        return cr_

    lax.fori_loop(0, OWN, own_fwd, 0)
    out(ptb, ptb_o, 2)
    pass_on(3)
    lax.fori_loop(0, OWN, own_dl, 0)
    out(dlt, dlt_o, 3)
    out(db_ref, db_o, 4)
    lax.fori_loop(0, OWN, dpool_block, 0)
    d2c = pltpu.make_async_remote_copy(src_ref=dpa.at[pl.ds((1 - c) * 2, 2)], dst_ref=d2d, send_sem=cs, recv_sem=cr,
                                       device_id={"dp": dpc}, device_id_type=MESH)
    d2c.start()
    d2c.wait()
    for h in range(2):
        d2d[h] = d2d[h] + dpa[c * 2 + h]
    out(d2d, own_o, 5)
    for k in range(4):
        cd = dpd * 4 + k
        if k % 2 == 0:
            rcopy(pall.at[cd], cd, sy.at[4 + k // 2], ry.at[4 + k // 2], dpy).wait_recv()
        else:
            rcopy(pall.at[cd], cd, sx.at[4 + k // 2], rx.at[4 + k // 2], dpx).wait_recv()
        relay(cd, sc.at[12 + k], rc.at[12 + k], dpc)
    for q, d in enumerate((dpx, dpy, dpd)):
        for k in range(4):
            ch = (d + 1 - 2 * c) * 4 + k
            i = q * 4 + 4 + k
            rcopy(pall.at[ch], ch, sc.at[i], rc.at[i], dpc).wait_recv()
    for cp in sends:
        cp.wait_send()
    for cp in locals_:
        cp.wait()


dma = pltpu.SemaphoreType.DMA
V = pltpu.VMEM
OWNR = OWN * RB


def spec(space):
    return pl.BlockSpec(memory_space=space)


def shape(*dims, dtype=F32):
    return jax.ShapeDtypeStruct(dims, dtype)


def block_scratch(n, lanes):
    return [V((HALF, lanes), BF16), V((OWN, HALF, RB), F32), V((WIDTH, lanes), BF16), V((2, 2, PROWS, LANE), F32),
            V((n, 8, RB), F32), V((n, PEERS + 1, 4, RB), F32), V((HALF, LANE), F32), V((LT, LANE), F32)]


def ln_gather(f_t, prm, w):
    return pl.pallas_call(
        ln_gather_kernel,
        out_shape=(shape(BATCH // LANE, PROWS, LANE), shape(ROWS, WIDTH), shape(7, ROWS, LANE), shape(1, RB),
                   shape(HALF, WIDTH, dtype=BF16), shape(HALF, LANE), shape(HALF, OWNR, dtype=BF16),
                   shape(WIDTH, OWNR, dtype=BF16), shape(HALF, LANE), shape(2, WIDTH, RB)),
        in_specs=[spec(pl.ANY), spec(V), spec(pl.ANY)],
        out_specs=(spec(pl.ANY),) + (spec(V),) * 3 + (spec(pl.ANY),) * 6,
        scratch_shapes=[V((2, TOKENS, SUB, WIDTH), BF16), V((LANE, WIDTH), F32), V((4, PROWS, LANE), F32),
                        V((WIDTH, HALF), BF16), V((TOKENS, SUB, LANE), F32), V((TOKENS, SUB, LANE), F32), V((SUB, WIDTH), F32),
                        V((HALF, WIDTH), BF16), V((HALF, LANE), F32)] + block_scratch(OWN, OWNR) +
                       [V((OWN, WIDTH, RB), F32), V((2, WIDTH, RB), F32),
                        dma((2,)), dma, dma((4,)), dma((6,)), dma((6,)), dma((16,)), dma((6,)), dma((6,)), dma((16,)),
                        dma((2, 2)), dma((OWN, PEERS)), dma((OWN, PEERS)), dma, dma, dma((6,))],
        compiler_params=pltpu.CompilerParams(collective_id=0, has_side_effects=True, vmem_limit_bytes=VMEM_ALL),
        name="ln_gather",
    )(f_t, prm, w)


def head_kernel(pall, wt_h, b_h, xhm_ref, dlt_h, ptb_h, db_h, own_h, loss0, dpool_ref, dwo, dwr, dbo, loss_ref, grad_ref,
                dlt, ering, ptb, pbuf, ylab, sbuf, db_ref, iota_ref, wt_ref, b_ref, d2d, dpa, ubuf, dbuf, dwt, gbuf,
                psem, ss, rs, us, ur, ds_, dr, dls, dss, dsr, bs, br, gs, gr, xsem, osem, lsem):
    z, dp, y, x, c = coords()
    dpc = dp + 1 - 2 * c

    bar = pltpu.get_barrier_semaphore()
    for j in range(PEERS):
        pl.semaphore_signal(bar, inc=1, device_id=peer(j), device_id_type=MESH)
        pl.semaphore_signal(bar, inc=1, device_id={"dp": lax.rem(dp + 1 + j, 8)}, device_id_type=MESH)

    ploads, fwd_block, dl_block = block_code(OWN, pall, wt_ref, b_ref, loss_ref, dlt, ering, ptb, pbuf, ylab, sbuf, db_ref,
                                             iota_ref, psem, ss, rs)
    own_lanes = slice(0, OWNR)
    loads = [pltpu.make_async_copy(src, dst, lsem.at[i]) for i, (src, dst) in enumerate((
        (own_h, d2d), (wt_h, wt_ref), (b_h, b_ref), (db_h, db_ref), (ptb_h, ptb.at[:, own_lanes]), (dlt_h, dlt.at[:, own_lanes])))]
    for cp in loads[0:2]:
        cp.start()
    for cp in ploads(OWN):
        cp.start()
    for cp in loads[2:]:
        cp.start()
    half = pl.multiple_of(c * HALF, LANE)
    iota_ref[...] = lax.broadcasted_iota(jnp.int32, (LT, LANE), 0).astype(F32)
    loss_ref[...] = loss0[...]
    loads[0].wait()
    pl.semaphore_wait(bar, 2 * PEERS)

    def part(j):
        return pl.ds(pl.multiple_of(j * ARW, ARW), ARW)

    def up(j):
        return pltpu.make_async_remote_copy(src_ref=ubuf.at[:, part(j), :], dst_ref=ubuf.at[:, part(j), :],
                                            send_sem=us.at[j], recv_sem=ur.at[j],
                                            device_id={"tp": jnp.minimum(z + 1, 3)}, device_id_type=MESH)

    def down(j):
        return pltpu.make_async_remote_copy(src_ref=dpa.at[:, part(j), :], dst_ref=dbuf.at[:, part(j), :],
                                            send_sem=ds_.at[j], recv_sem=dr.at[j],
                                            device_id={"tp": jnp.maximum(z - 1, 0)}, device_id_type=MESH)

    @pl.when(z == 0)
    def _():
        for j in range(ARC):
            ubuf[:, part(j), :] = d2d[:, part(j), :]
            up(j).start()

    @pl.when(z == 3)
    def _():
        for j in range(ARC):
            dpa[:, part(j), :] = d2d[:, part(j), :]
            down(j).start()

    def tick(t):
        j = t - 2 * z

        @pl.when((z >= 1) & (j >= 0) & (j < ARC))
        def _():
            up(j).wait_recv()
            ubuf[:, part(j), :] += d2d[:, part(j), :]

            @pl.when(z < 3)
            def _():
                up(j).start()

        k = t - 2 * (3 - z)

        @pl.when((z <= 2) & (k >= 0) & (k < ARC))
        def _():
            down(k).wait_recv()

            @pl.when(z > 0)
            def _():
                dpa[:, part(k), :] = dbuf[:, part(k), :] + d2d[:, part(k), :]
                down(k).start()

    for cp in loads[1:4]:
        cp.wait()

    def rest(r, cr_):
        fwd_block(r, NB)

        @pl.when(r >= OWN + 2)
        def _():
            dl_block(r - 2)

        tick(r - OWN)
        return cr_

    def last_dl(r, cr_):
        dl_block(r)
        return cr_

    lax.fori_loop(OWN, NB, rest, 0)
    lax.fori_loop(NB - 2, NB, last_dl, 0)
    for cp in loads[4:]:
        cp.wait()

    for n in range(NT):
        row = jnp.sum(db_ref[n * TILE:(n + 1) * TILE, :].T, axis=0, keepdims=True)
        dbo[0:1, pl.ds(pl.multiple_of(half + n * TILE, 128), TILE)] = row
    dbc = pltpu.make_async_remote_copy(src_ref=dbo.at[:, pl.ds(half, HALF)], dst_ref=dbo.at[:, pl.ds(half, HALF)], send_sem=bs, recv_sem=br,
                                       device_id={"dp": dpc}, device_id_type=MESH)
    dbc.start()

    xcopies = [pltpu.make_async_copy(xhm_ref.at[:, q * RB:(q + 1) * RB], ering.at[0, q * ROWS:(q + 1) * ROWS, :], xsem.at[q])
               for q in range(3)]
    for cp in xcopies:
        cp.start()

    def dw_local(n):
        slot = lax.rem(n, 2)
        return pltpu.make_async_copy(dwt.at[slot], dwo.at[:, pl.ds(pl.multiple_of(n * TILE, TILE), TILE)], dls.at[slot])

    def dw_remote(n):
        slot = lax.rem(n, 2)
        return pltpu.make_async_remote_copy(
            src_ref=dwt.at[slot], dst_ref=dwr.at[:, pl.ds(pl.multiple_of(n * TILE, TILE), TILE)],
            send_sem=dss.at[slot], recv_sem=dsr.at[n], device_id={"dp": dpc}, device_id_type=MESH)

    def dw_step(n, cr_):
        @pl.when(n >= 2)
        def _():
            dw_local(n - 2).wait()
            dw_remote(n - 2).wait_send()

        rows = pl.ds(pl.multiple_of(n * TILE, TILE), TILE)
        dwt[lax.rem(n, 2)] = lax.dot_general(ptb[...], dlt[rows, :], (((1,), (1,)), ((), ())), preferred_element_type=F32)
        dw_local(n).start()
        dw_remote(n).start()
        tick(n + NB - OWN)
        return cr_

    lax.fori_loop(0, NT, dw_step, 0)

    for cp in xcopies:
        cp.wait()
    for j in range(WIDTH // LANE):
        rows = slice(j * LANE, (j + 1) * LANE)
        tot = jnp.where(z < 3, dbuf[:, rows, :], 0.0) + ubuf[:, rows, :]
        tt = jnp.concatenate([tot[0], tot[1]], axis=1).T
        q, lo = j // 2, (j % 2) * 128
        ering[1, q * ROWS:(q + 1) * ROWS, lo:lo + 128] = tt
        cols = slice(j * 128, (j + 1) * 128)
        gbuf[7, 0:1, cols] = jnp.sum(tt * ering[0, q * ROWS:(q + 1) * ROWS, lo:lo + 128], axis=0, keepdims=True)
        gbuf[7, 1:2, cols] = jnp.sum(tt, axis=0, keepdims=True)
    ocopies = [pltpu.make_async_copy(ering.at[1, q * ROWS:(q + 1) * ROWS, :], dpool_ref.at[:, q * RB:(q + 1) * RB], osem.at[q])
               for q in range(3)]
    for cp in ocopies:
        cp.start()

    def gcopy(j, slot):
        return pltpu.make_async_remote_copy(src_ref=gbuf.at[7], dst_ref=gbuf.at[slot], send_sem=gs.at[j], recv_sem=gr.at[slot],
                                            device_id={"dp": lax.rem(dp + 1 + j, 8)}, device_id_type=MESH)

    for j in range(PEERS):
        gcopy(j, 6 - j).start()

    for n in (NT - 2, NT - 1):
        dw_local(n).wait()
        dw_remote(n).wait_send()

    def dw_recv(n, cr_):
        dw_remote(n).wait_recv()
        return cr_

    lax.fori_loop(0, NT, dw_recv, 0)
    dbc.wait_send()
    other = pl.ds(pl.multiple_of((1 - c) * HALF, 128), HALF)
    pltpu.make_async_remote_copy(src_ref=dbo.at[:, other], dst_ref=dbo.at[:, other], send_sem=bs, recv_sem=br,
                                 device_id={"dp": dpc}, device_id_type=MESH).wait_recv()
    for j in range(PEERS):
        gcopy(j, j).wait_recv()
        gcopy(j, j).wait_send()
    for cp in ocopies:
        cp.wait()
    grads = gbuf[7]
    for j in range(PEERS):
        grads = grads + gbuf[j]
    grad_ref[...] = grads

    @pl.when(z < 3)
    def _():
        for j in range(ARC):
            up(j).wait_send()

    @pl.when(z > 0)
    def _():
        for j in range(ARC):
            down(j).wait_send()


def head(pall, wt, bb, xhm, dlt, ptb, db, own, loss):
    return pl.pallas_call(
        head_kernel,
        out_shape=(shape(ROWS, WIDTH), shape(WIDTH, HALF), shape(WIDTH, HALF), shape(1, CLS), shape(1, RB), shape(2, WIDTH)),
        in_specs=[spec(pl.ANY)] * 8 + [spec(V)],
        out_specs=(spec(pl.ANY),) * 3 + (spec(V),) * 3,
        scratch_shapes=block_scratch(NB - OWN, BATCH) +
                       [V((HALF, WIDTH), BF16), V((HALF, LANE), F32)] + [V((2, WIDTH, RB), F32)] * 4 +
                       [V((2, WIDTH, TILE), F32), V((PEERS + 1, 2, WIDTH), F32),
                        dma((2, 2)), dma((NB - OWN, PEERS)), dma((NB - OWN, PEERS)),
                        dma((ARC,)), dma((ARC,)), dma((ARC,)), dma((ARC,)),
                        dma((2,)), dma((2,)), dma((NT,)), dma, dma, dma((PEERS,)), dma((PEERS,)), dma((3,)), dma((3,)), dma((6,))],
        compiler_params=pltpu.CompilerParams(collective_id=1, has_side_effects=True, vmem_limit_bytes=VMEM_ALL),
        name="head",
    )(pall, wt, bb, xhm, dlt, ptb, db, own, loss)


DROWS = WIDTH // (ROWS // SUB)


def ln_bwd_kernel(f_ref, stat_ref, dp_ref, prm, dwo, dwr, o_ref, dw_ref, mb, ib, kb, ub, cbuf, ls, ws):
    c = lax.rem(lax.axis_index("dp"), 2)
    i = pl.program_id(0)
    last = ROWS // SUB - 1

    def pull(i):
        slot = lax.rem(i, 2)
        rows = pl.ds(pl.multiple_of(i * DROWS, 8), DROWS)
        return [pltpu.make_async_copy(h.at[rows, :], cbuf.at[slot, q], ls.at[slot, q]) for q, h in enumerate((dwo, dwr))]

    def push(i):
        slot = lax.rem(i, 2)
        rows = pl.ds(pl.multiple_of(i * DROWS, 8), DROWS)
        return [pltpu.make_async_copy(cbuf.at[slot, q], dw_ref.at[rows, pl.ds(pl.multiple_of((c + q - 2 * c * q) * HALF, 128), HALF)],
                                      ws.at[slot, q]) for q in range(2)]

    @pl.when(i >= 2)
    def _():
        for cp in push(i - 2):
            cp.wait()

    for cp in pull(i):
        cp.start()

    @pl.when(i >= 1)
    def _():
        for cp in pull(i - 1):
            cp.wait()
        for cp in push(i - 1):
            cp.start()

    u = dp_ref[...] * prm[1:2, :] * (1.0 / TOKENS)
    ub[...] = u - jnp.sum(u, axis=-1, keepdims=True) * (1.0 / WIDTH)

    def spread(g):
        st = stat_ref[g]
        for j in range(TG):
            mb[g * TG + j] = jnp.broadcast_to(st[:, j:j + 1], (SUB, LANE))
            ib[g * TG + j] = jnp.broadcast_to(st[:, SIDE + j:SIDE + j + 1], (SUB, LANE))

    def project(g):
        for j in range(TG):
            t = g * TG + j
            d = f_ref[t].astype(F32) - rep(mb[t])
            inv = ib[t]
            kb[t] = (inv * inv * inv) * (jnp.sum(d * ub[...], axis=-1, keepdims=True) * (1.0 / WIDTH))

    def write(g):
        for j in range(TG):
            t = g * TG + j
            d = f_ref[t].astype(F32) - rep(mb[t])
            o_ref[t] = (rep(ib[t]) * ub[...] - rep(kb[t]) * d).astype(BF16)

    spread(0)
    spread(1)
    project(0)

    def body(g, cr_):
        write(g - 1)
        project(g)
        spread(g + 1)
        return cr_

    lax.fori_loop(1, 6, body, 0)
    write(5)
    project(6)
    write(6)

    @pl.when(i == last)
    def _():
        for cp in pull(i):
            cp.wait()
        for cp in push(i):
            cp.start()
        for cp in push(i - 1):
            cp.wait()
        for cp in push(i):
            cp.wait()


def ln_bwd(f_t, stat, dpool, prm, dwo, dwr):
    blk = pl.BlockSpec((TOKENS, SUB, WIDTH), lambda i: (0, i, 0))
    hbm = spec(pl.ANY)
    return pl.pallas_call(
        ln_bwd_kernel,
        grid=(ROWS // SUB,),
        out_shape=(jax.ShapeDtypeStruct((TOKENS, ROWS, WIDTH), BF16), jax.ShapeDtypeStruct((WIDTH, CLS), F32)),
        in_specs=[blk, pl.BlockSpec((7, SUB, 128), lambda i: (0, i, 0)),
                  pl.BlockSpec((SUB, WIDTH), lambda i: (i, 0)), pl.BlockSpec((8, WIDTH), lambda i: (0, 0)), hbm, hbm],
        out_specs=(blk, hbm),
        scratch_shapes=[V((TOKENS, SUB, 128), F32), V((TOKENS, SUB, 128), F32), V((TOKENS, SUB, 128), F32), V((SUB, WIDTH), F32),
                        V((2, 2, DROWS, HALF), F32), pltpu.SemaphoreType.DMA((2, 2)), pltpu.SemaphoreType.DMA((2, 2))],
        name="ln_bwd",
    )(f_t, stat, dpool, prm, dwo, dwr)


def solution(mesh):
    def local(feats, gamma, beta, w, b, labels):
        f_t = jnp.transpose(feats, (1, 0, 2))

        def row(v):
            return jnp.pad(v.astype(F32), (0, CLS - v.shape[0]))

        zero = jnp.zeros((CLS,), F32)
        prm = jnp.stack([b, row(gamma), row(beta), row(labels), zero, zero, zero, zero])
        pall, xhm, stat, loss, wt, bb, dlt, ptb, db, own = ln_gather(f_t, prm, w)
        dpool, dwo, dwr, db, loss, grads = head(pall, wt, bb, xhm, dlt, ptb, db, own, loss)
        df_t, dw = ln_bwd(f_t, stat, dpool, prm, dwo, dwr)
        return jnp.sum(loss) / BATCH, jnp.transpose(df_t, (1, 0, 2)), dw, db[0], grads[0], grads[1]

    return jax.shard_map(local, mesh=mesh, in_specs=(P("dp", None, None), P(), P(), P(None, "tp"), P("tp"), P("dp")),
                         out_specs=(P(), P("dp", None, None), P(None, "tp"), P("tp"), P(), P()), check_vma=False)
```

time: 426 us -> 243 us (0.57)
  Pallas kernels: 0 us -> 233 us
  waiting for transfers between devices: 208 us -> 0 us
  other arithmetic: 109 us -> 2.58 us
  blocking collectives: 47.7 us -> 0 us
  matrix products: 30.8 us -> 0 us
  between operations: 16 us -> 2.49 us
  local copies, waits for them, and re-layouts: 14.3 us -> 3.69 us
    pallas_call x0 -> x3, Pallas kernels: none -> 233 us  [the longest x1 108 us: head(): pl.pallas_call(head_kernel, out_shape=(shape(ROWS, WIDTH), shape(WIDTH, H...]
    psum x2 -> x0, waiting for transfers between devices: 208 us -> none  [the longest x1 151 us: local_head(): lax.psum(lax.dot_general(pooled16, dlogit16, (((0,), (0,)), ((), ())), pr...]
    reduce_sum x8 -> x1, other arithmetic: 81.8 us -> 1.23 us  [local(): jnp.sum(loss) / BATCH]
    psum x2 -> x0, blocking collectives: 34.3 us -> none  [the longest x1 25.7 us: local_head(): lax.psum((jnp.sum(loss_rows), grad_gamma, grad_beta), 'dp')]
    dot_general x3 -> x0, matrix products: 30.8 us -> none  [the longest x1 11.4 us: local_head(): lax.dot_general(pooled16, dlogit16, (((0,), (0,)), ((), ())), preferred_e...]
    convert_element_type x1, other arithmetic: 26.2 us -> 0.69 us  [row(): return jnp.pad(v.astype(F32), (0, CLS - v.shape[0]))]
    unnamed x11 -> x4, local copies, waits for them, and re-layouts: 14.3 us -> 0.01 us
    pmax x1 -> x0, blocking collectives: 13.5 us -> none  [local_head(): row_max = lax.pmax(jnp.max(logits, axis=-1), 'tp')]
  transfers between devices with their start and end apart: 2 -> 0, of which waited for: 2 -> 0; matrix products, arithmetic and copies ran while one was open for 14% -> 0% of each run, Pallas kernels for 0% -> 0%
where the time goes in v2:
time: 243 us; the launch traced here: 242 us
  Pallas kernels  233 us (96%)
  local copies, waits for them, and re-layouts  3.69 us (2%)
  other arithmetic  2.58 us (1%)
  between operations  2.49 us (1%)
    pallas_call x1, Pallas kernels, head(): pl.pallas_call(head_kernel, out_shape=(shape(ROWS, WIDTH), shape(WIDTH, H...  108 us
    pallas_call x1, Pallas kernels, ln_gather(): pl.pallas_call(ln_gather_kernel, out_shape=(shape(BATCH // LANE, PROWS, L...  75 us
    pallas_call x1, Pallas kernels, ln_bwd(): pl.pallas_call(ln_bwd_kernel, grid=(ROWS // SUB,), out_shape=(jax.ShapeDt...  50.4 us

profile of v2, /device:TPU:0, one launch (start us, length us, event | category | flops | bytes accessed | tf_op | source)
XLA Modules:
  0.0 242.2 jit_solution(13327903801195709523)
XLA Ops:
  0.6 0.8 stack.18
  1.4 0.7 pad.11
  2.1 0.7 pad.12
  2.8 0.7 convert_element_type.8
  3.6 0.8 stack.23.prm
  4.4 75.0 %ln_gather.1 = (f32[32,776,128]{2,1,0:T(8,128)}, f32[512,768]{1,0:T(8,128)}, f32[7,512,128]{2,1,0:T(8,128)}, f32[1,256]{1,0:T(1,128)}, bf16[2816,768]{1,0:T(8,12...) custom-call(bf16[49,512,768]{2,1,0:T(8,128)(2,1)} %bitcast.2, ...), custom_call_target="tpu_custom_call" | custom-call | tf_op jit(solution)/shard_map/ln_gather/pallas_call | solution.py:403
  79.4 108.0 %head.1 = (f32[512,768]{1,0:T(8,128)}, f32[768,2816]{1,0:T(8,128)}, f32[768,2816]{1,0:T(8,128)}, f32[1,5632]{1,0:T(1,128)}, f32[1,256]{1,0:T(1,128)}, /*index=5*/f32[2,768]{1,0:T(2,128)}) custom-call(f32[32,776,128]{2,1,0:T(8,128)} %get-tuple-element.24.pall, bf16[2816,768]{1,0:T(8,128)(2,1)} %get-tuple-element.25.wt_h, f32[2816,128]{1,0:T(8,128)} %get-tuple-element.26.b_h, ...), custom_call_target="tpu_custom_call" | custom-call | tf_op jit(solution)/shard_map/head/pallas_call | solution.py:614
  187.5 1.2 reduce_sum.9
  189.3 0.0 copy-start
  189.3 0.0 copy-start.1
  189.4 50.4 %ln_bwd.1 = (bf16[49,512,768]{2,1,0:T(8,128)(2,1)}, f32[768,5632]{1,0:T(8,128)}) custom-call(bf16[49,512,768]{2,1,0:T(8,128)(2,1)} %bitcast.3, f32[7,512,128]{2,1,0:T(8,128)} %get-tuple-element.34.stat_ref, f32[512,768]{1,0:T(8,128)} %get-tuple-element.35.dp_ref, f32[8,5632]{1,0:T(8,128)} %stack.23.prm, f32[768,2816]{1,0:T(8,128)} %get-tuple-element.36.dwo, ...), custom_call_target="tpu_custom_call" | custom-call | tf_op jit(solution)/shard_map/ln_bwd/pallas_call | solution.py:716
  239.8 0.0 copy-done
  239.8 0.7 reduce
  240.4 0.0 copy-done.1
  240.4 0.6 slice_reduce_fusion
  (5 shorter events, 0.1 us)
Async XLA Ops:
  189.3 50.4 %copy-start = (f32[1,5632]{1,0:T(1,128)S(1)}, f32[1,5632]{1,0:T(1,128)}, u32[]{:S(2)}) copy-start(f32[1,5632]{1,0:T(1,128)} %get-tuple-element.40) | copy-start | bytes 67588
  189.3 51.1 %copy-start.1 = (f32[2,768]{1,0:T(2,128)S(1)}, f32[2,768]{1,0:T(2,128)}, u32[]{:S(2)}) copy-start(f32[2,768]{1,0:T(2,128)} %get-tuple-element.41) | copy-start | bytes 18436

commit v3 on v2

--- a/solution.py
+++ b/solution.py
@@ -26,6 +26,7 @@
 ARW = 64
 ARC = WIDTH // ARW
 LANE = 128
+LAG = 3
 TG = 7
 SIDE = 64
 PEERS = 7
@@ -88,8 +89,10 @@
         return pltpu.make_async_remote_copy(src_ref=sbuf.at[i, PEERS], dst_ref=sbuf.at[i, slot], send_sem=ss.at[i, j],
                                             recv_sem=rs.at[i, slot], device_id=peer(j), device_id_type=MESH)
 
-    def fwd_block(r, stop):
+    def fwd_block(r, stop, fused=0):
         slot = lax.rem(r, 2)
+        if fused:
+            dl_tile = dl_stats(r - LAG)
 
         @pl.when(r + 1 < stop)
         def _():
@@ -107,6 +110,9 @@
         mx, tg, vs = jnp.full((8, RB), -3e38, F32), zero, zero
         for n in range(HALF // LT):
             full = jnp.dot(wt_ref[n * LT:(n + 1) * LT, :], ptb[:, lanes], preferred_element_type=F32)
+            if fused:
+                dl_tile(2 * n, 0)
+                dl_tile(2 * n + 1, n)
             for lo, size, masked in (((0, LT, 0),) if n == 0 else ((0, ET, 0), (ET, ET, 1))):
                 row = n * LT + lo
                 bb = b_ref[row:row + size, :]
@@ -136,7 +142,7 @@
         for j in range(PEERS):
             scopy(r, j, PEERS - 1 - j).start()
 
-    def dl_block(r):
+    def dl_stats(r):
         es = lax.rem(r, OWN)
         for j in range(PEERS):
             cp = scopy(r, j, j)
@@ -158,12 +164,17 @@
         lanes = pl.ds(pl.multiple_of(r * RB, RB), RB)
 
         def tile(n, masked):
-            rows = pl.ds(pl.multiple_of(n * ET, ET), ET)
+            rows = slice(n * ET, n * ET + ET) if isinstance(n, int) else pl.ds(pl.multiple_of(n * ET, ET), ET)
             off = lax.convert_element_type(n * ET, F32)
             base = jnp.where(ids(ET) < limit_f - off, C0, 0.0) if masked else C0
             d = ering[es, rows, :] * scb - jnp.where(ids(ET) == shifted(yb, off, ET), C1, base)
             db_ref[rows, :] += d[:, 0:LANE] + d[:, LANE:RB]
             dlt[rows, lanes] = d.astype(BF16)
+
+        return tile
+
+    def dl_block(r):
+        tile = dl_stats(r)
 
         def plain(n, cr_):
             tile(n, 0)
@@ -459,25 +470,19 @@
                                             send_sem=ds_.at[j], recv_sem=dr.at[j],
                                             device_id={"tp": jnp.maximum(z - 1, 0)}, device_id_type=MESH)
 
-    @pl.when(z == 0)
-    def _():
-        for j in range(ARC):
-            ubuf[:, part(j), :] = d2d[:, part(j), :]
-            up(j).start()
-
-    @pl.when(z == 3)
-    def _():
-        for j in range(ARC):
-            dpa[:, part(j), :] = d2d[:, part(j), :]
-            down(j).start()
-
     def tick(t):
         j = t - 2 * z
 
-        @pl.when((z >= 1) & (j >= 0) & (j < ARC))
+        @pl.when((j >= 0) & (j < ARC))
         def _():
-            up(j).wait_recv()
-            ubuf[:, part(j), :] += d2d[:, part(j), :]
+            @pl.when(z == 0)
+            def _():
+                ubuf[:, part(j), :] = d2d[:, part(j), :]
+
+            @pl.when(z > 0)
+            def _():
+                up(j).wait_recv()
+                ubuf[:, part(j), :] += d2d[:, part(j), :]
 
             @pl.when(z < 3)
             def _():
@@ -485,25 +490,29 @@
 
         k = t - 2 * (3 - z)
 
-        @pl.when((z <= 2) & (k >= 0) & (k < ARC))
+        @pl.when((k >= 0) & (k < ARC))
         def _():
-            down(k).wait_recv()
+            @pl.when(z == 3)
+            def _():
+                dpa[:, part(k), :] = d2d[:, part(k), :]
+
+            @pl.when(z < 3)
+            def _():
+                down(k).wait_recv()
+
+            @pl.when((z > 0) & (z < 3))
+            def _():
+                dpa[:, part(k), :] = dbuf[:, part(k), :] + d2d[:, part(k), :]
 
             @pl.when(z > 0)
             def _():
-                dpa[:, part(k), :] = dbuf[:, part(k), :] + d2d[:, part(k), :]
                 down(k).start()
 
     for cp in loads[1:4]:
         cp.wait()
 
-    def rest(r, cr_):
-        fwd_block(r, NB)
-
-        @pl.when(r >= OWN + 2)
-        def _():
-            dl_block(r - 2)
-
+    def rest(fused, r, cr_):
+        fwd_block(r, NB, fused)
         tick(r - OWN)
         return cr_
 
@@ -511,8 +520,9 @@
         dl_block(r)
         return cr_
 
-    lax.fori_loop(OWN, NB, rest, 0)
-    lax.fori_loop(NB - 2, NB, last_dl, 0)
+    lax.fori_loop(OWN, OWN + LAG, functools.partial(rest, 0), 0)
+    lax.fori_loop(OWN + LAG, NB, functools.partial(rest, 1), 0)
+    lax.fori_loop(NB - LAG, NB, last_dl, 0)
     for cp in loads[4:]:
         cp.wait()
 
@@ -548,10 +558,15 @@
         dwt[lax.rem(n, 2)] = lax.dot_general(ptb[...], dlt[rows, :], (((1,), (1,)), ((), ())), preferred_element_type=F32)
         dw_local(n).start()
         dw_remote(n).start()
-        tick(n + NB - OWN)
+
+        @pl.when(lax.rem(n, 2) == 1)
+        def _():
+            tick(NB - OWN + n // 2)
+
         return cr_
 
     lax.fori_loop(0, NT, dw_step, 0)
+    tick(NB - OWN + NT // 2)
 
     for cp in xcopies:
         cp.wait()

time: 243 us -> 212 us (0.87)
  Pallas kernels: 233 us -> 203 us
    pallas_call x1, Pallas kernels: 108 us -> 77.3 us  [head(): pl.pallas_call(head_kernel, out_shape=(shape(ROWS, WIDTH), shape(WIDTH, H...]
where the time goes in v3:
time: 212 us; the launch traced here: 211 us
  Pallas kernels  203 us (96%)
  local copies, waits for them, and re-layouts  3.69 us (2%)
  other arithmetic  2.58 us (1%)
  between operations  2.49 us (1%)
    pallas_call x1, Pallas kernels, head(): pl.pallas_call(head_kernel, out_shape=(shape(ROWS, WIDTH), shape(WIDTH, H...  77.3 us
    pallas_call x1, Pallas kernels, ln_gather(): pl.pallas_call(ln_gather_kernel, out_shape=(shape(BATCH // LANE, PROWS, L...  75 us
    pallas_call x1, Pallas kernels, ln_bwd(): pl.pallas_call(ln_bwd_kernel, grid=(ROWS // SUB,), out_shape=(jax.ShapeDt...  50.4 us

profile of v3, /device:TPU:0, one launch (start us, length us, event | category | flops | bytes accessed | tf_op | source)
XLA Modules:
  0.0 211.4 jit_solution(5599325367759214270)
XLA Ops:
  0.6 0.8 stack.18
  1.4 0.7 pad.11
  2.1 0.7 pad.12
  2.8 0.7 convert_element_type.8
  3.6 0.8 stack.23.prm
  4.4 75.0 %ln_gather.1 = (f32[32,776,128]{2,1,0:T(8,128)}, f32[512,768]{1,0:T(8,128)}, f32[7,512,128]{2,1,0:T(8,128)}, f32[1,256]{1,0:T(1,128)}, bf16[2816,768]{1,0:T(8,12...) custom-call(bf16[49,512,768]{2,1,0:T(8,128)(2,1)} %bitcast.2, ...), custom_call_target="tpu_custom_call" | custom-call | tf_op jit(solution)/shard_map/ln_gather/pallas_call | solution.py:414
  79.4 77.3 %head.1 = (f32[512,768]{1,0:T(8,128)}, f32[768,2816]{1,0:T(8,128)}, f32[768,2816]{1,0:T(8,128)}, f32[1,5632]{1,0:T(1,128)}, f32[1,256]{1,0:T(1,128)}, /*index=5*/f32[2,768]{1,0:T(2,128)}) custom-call(f32[32,776,128]{2,1,0:T(8,128)} %get-tuple-element.24.pall, bf16[2816,768]{1,0:T(8,128)(2,1)} %get-tuple-element.25.wt_h, f32[2816,128]{1,0:T(8,128)} %get-tuple-element.26.b_h, ...), custom_call_target="tpu_custom_call" | custom-call | tf_op jit(solution)/shard_map/head/pallas_call | solution.py:629
  156.7 1.2 reduce_sum.9
  158.6 0.0 copy-start
  158.6 0.0 copy-start.1
  158.6 50.4 %ln_bwd.1 = (bf16[49,512,768]{2,1,0:T(8,128)(2,1)}, f32[768,5632]{1,0:T(8,128)}) custom-call(bf16[49,512,768]{2,1,0:T(8,128)(2,1)} %bitcast.3, f32[7,512,128]{2,1,0:T(8,128)} %get-tuple-element.34.stat_ref, f32[512,768]{1,0:T(8,128)} %get-tuple-element.35.dp_ref, f32[8,5632]{1,0:T(8,128)} %stack.23.prm, f32[768,2816]{1,0:T(8,128)} %get-tuple-element.36.dwo, ...), custom_call_target="tpu_custom_call" | custom-call | tf_op jit(solution)/shard_map/ln_bwd/pallas_call | solution.py:731
  209.0 0.0 copy-done
  209.0 0.7 reduce
  209.6 0.0 copy-done.1
  209.6 0.6 slice_reduce_fusion
  (5 shorter events, 0.1 us)
Async XLA Ops:
  158.6 50.4 %copy-start = (f32[1,5632]{1,0:T(1,128)S(1)}, f32[1,5632]{1,0:T(1,128)}, u32[]{:S(2)}) copy-start(f32[1,5632]{1,0:T(1,128)} %get-tuple-element.40) | copy-start | bytes 67588
  158.6 51.1 %copy-start.1 = (f32[2,768]{1,0:T(2,128)S(1)}, f32[2,768]{1,0:T(2,128)}, u32[]{:S(2)}) copy-start(f32[2,768]{1,0:T(2,128)} %get-tuple-element.41) | copy-start | bytes 18436
